TPU v7x, 32 devices: a whole 2x2x4 slice. The times are simulated.
32 devices in a mesh: dp: 16 (over z, x, core), rep: 2 (over y).
Axes of the slice: x: 2, y: 2, z: 4, core: 2. Of those that a mesh axis runs over, the one named last changes fastest.
Arguments:
- tokens: bfloat16 [48, 261, 768], P('dp'), may hold values from -6 to 6
- text_len: int32 [48], P('dp'), may hold values from 1 to 64, as said below
- routes: int32 [48, 261], P('dp'), may hold values from 0 to 2, as said below
- attn_gain: float32 [768], replicated, may hold values from 0.5 to 1.5
- attn_shift: float32 [768], replicated, may hold values from -1 to 1
- w_qkv: bfloat16 [3, 768, 768], P(None, 'dp', 'rep'), may hold values from -0.21875 to 0.21875
- b_qv: float32 [2, 768], P(None, 'rep'), may hold values from -1.5 to 1.5
- w_out: bfloat16 [768, 768], P('dp', 'rep'), may hold values from -1.25 to 1.25
- b_out: float32 [768], replicated, may hold values from -0.5 to 0.5
- ffn_gain: float32 [768], replicated, may hold values from 0.5 to 1.5
- ffn_shift: float32 [768], replicated, may hold values from -1 to 1
- w_up: bfloat16 [3, 768, 3072], P(None, 'dp', 'rep'), may hold values from -0.21875 to 0.21875
- b_up: float32 [3, 3072], P(None, 'rep'), may hold values from -1.5 to 1.5
- w_down: bfloat16 [3, 768, 3072], P(None, 'dp', 'rep'), may hold values from -0.15625 to 0.15625
- b_down: float32 [3, 768], replicated, may hold values from -0.5 to 0.5
- cotangent: bfloat16 [48, 261, 768], P('dp'), may hold values from -6 to 6
Outputs:
- output: bfloat16 [48, 261, 768], P('dp')
- grad_tokens: float32 [48, 261, 768], P('dp')
- grad_w_qkv: float32 [3, 768, 768], P(None, 'dp', 'rep')
- grad_w_out: float32 [768, 768], P('dp', 'rep')
- grad_w_up: float32 [3, 768, 3072], P(None, 'dp', 'rep')
- grad_w_down: float32 [3, 768, 3072], P(None, 'dp', 'rep')
- grad_b_qv: float32 [2, 768], P(None, 'rep')
- grad_b_out: float32 [768], replicated
- grad_b_up: float32 [3, 3072], P(None, 'rep')
- grad_b_down: float32 [3, 768], replicated
- grad_norms: float32 [4, 768], replicated
Inputs may be any that keep to these rules, and one draw needn't show every extreme that they name: `text_len`: text rows in use of each item; some item uses all 64 in every draw. `routes`: routing by modality: each item either sends its first 197 rows to expert 0 and its other rows to expert 1, or sends all its rows to expert 2; both kinds of item occur in every draw.
All inputs are finite; a program needn't handle non-finite values.
Results may differ from a plain program's by a relative error of at most 0.014.
Values may be sent and summed in bfloat16 or wider, within the bound.
No kernel may reach another device: no remote copies, remote signals or barrier semaphores. Data moves between devices by JAX's collectives and lax.ppermute only.
A program may use at most 192 MiB of HBM per device.

v0:
```python
import functools
import math

import jax
import jax.numpy as jnp
from jax import lax
from jax.experimental import pallas as pl
from jax.experimental.pallas import tpu as pltpu
from jax.sharding import PartitionSpec as P

HDIM = 64
IMG = 197
EPSILON = 1e-05
ROOT_HALF = 0.7071067811865476
INV_ROOT_TAU = 0.3989422804014327
SUB = 16
LANES = 128
BF = jnp.bfloat16
F32 = jnp.float32

NN = (((1,), (0,)), ((), ()))
NT = (((1,), (1,)), ((), ()))
TN = (((0,), (0,)), ((), ()))


def up_to(n, m):
    return -(-n // m) * m


def dot(a, b, dims):
    return lax.dot_general(a, b, dims, preferred_element_type=F32)


def full(shape):
    zeros = (0,) * len(shape)
    return pl.BlockSpec(shape, lambda *_: zeros)


def per_item(shape):
    zeros = (0,) * (len(shape) - 1)
    return pl.BlockSpec(shape, lambda i, *_: (i,) + zeros)


ANY = pl.BlockSpec(memory_space=pl.ANY)


def params():
    return pltpu.CompilerParams(vmem_limit_bytes=60 * 1024 * 1024)


SHORT = pl.CostEstimate(flops=1, transcendentals=0, bytes_accessed=1)


def normed(v):
    centred = v - jnp.mean(v, axis=-1, keepdims=True)
    var = jnp.mean(centred * centred, axis=-1, keepdims=True)
    spread = lax.rsqrt(var + EPSILON)
    return centred * spread, spread


def norm_back(grad, hat, spread, gain):
    scaled = grad * gain
    return spread * (
        scaled
        - jnp.mean(scaled, axis=-1, keepdims=True)
        - hat * jnp.mean(scaled * hat, axis=-1, keepdims=True)
    )


def run_copies(copies, *, start=False, wait=False):
    for c in copies:
        if start:
            c.start()
        if wait:
            c.wait()


def place_copies(off_ref, pieces, dest, sems, plane=0):
    copies = []
    for n, piece in enumerate(pieces):
        subs, _, rows, _ = piece.shape
        for j in range(subs):
            at = off_ref[n * subs + j]
            copies.append(
                pltpu.make_async_copy(
                    piece.at[j, plane : plane + dest.shape[0]],
                    dest.at[:, pl.ds(pl.multiple_of(at, SUB), rows), :],
                    sems.at[n * subs + j],
                )
            )
    return copies


def k_proj(off_ref, tok_ref, vec_ref, bias_ref, *rest):
    a_ref, qkv_ref, w_ref, wo_ref, sems, out_sems = rest[-6:]
    pieces = rest[:-6]
    first = pl.program_id(0) == 0

    @pl.when(first)
    def _():
        run_copies(place_copies(off_ref, pieces, w_ref, sems), start=True)
        run_copies(place_copies(off_ref, pieces, wo_ref, out_sems, 3), start=True)

    hat, _ = normed(tok_ref[0].astype(F32))
    a_ref[0] = (hat * vec_ref[0:1, :] + vec_ref[1:2, :]).astype(BF)

    @pl.when(first)
    def _():
        run_copies(place_copies(off_ref, pieces, w_ref, sems), wait=True)
        run_copies(place_copies(off_ref, pieces, wo_ref, out_sems, 3), wait=True)

    a = a_ref[0]
    for t in range(3):
        qkv_ref[t, 0] = (dot(a, w_ref[t], NN) + bias_ref[t : t + 1, :]).astype(BF)


def project(tokens, vectors, bias, pieces, offsets):
    items, rows, width = tokens.shape
    cols = pieces[0].shape[3]
    count = len(pieces) * pieces[0].shape[0]
    grid_spec = pltpu.PrefetchScalarGridSpec(
        num_scalar_prefetch=1,
        grid=(items,),
        in_specs=[
            per_item((1, rows, width)),
            full(vectors.shape),
            full((3, cols)),
        ]
        + [ANY] * len(pieces),
        out_specs=[
            per_item((1, rows, width)),
            pl.BlockSpec((3, 1, rows, cols), lambda i, *_: (0, i, 0, 0)),
            full((3, width, cols)),
            full((1, width, cols)),
        ],
        scratch_shapes=[pltpu.SemaphoreType.DMA((count,)), pltpu.SemaphoreType.DMA((count,))],
    )
    return pl.pallas_call(
        k_proj,
        grid_spec=grid_spec,
        out_shape=[
            jax.ShapeDtypeStruct((items, rows, width), BF),
            jax.ShapeDtypeStruct((3, items, rows, cols), BF),
            jax.ShapeDtypeStruct((3, width, cols), BF),
            jax.ShapeDtypeStruct((1, width, cols), BF),
        ],
        compiler_params=params(),
        cost_estimate=SHORT,
        name="project",
    )(offsets, tokens, vectors, bias, *pieces)


def k_attend(len_ref, q_ref, k_ref, v_ref, c_ref, *, scale):
    rows, width = c_ref.shape[1:]
    length = len_ref[pl.program_id(0)]
    valid = lax.broadcasted_iota(jnp.int32, (1, rows), 1) < IMG + length
    low = lax.broadcasted_iota(jnp.int32, (1, LANES), 1) < HDIM
    for pair in range(width // LANES):
        cols = slice(pair * LANES, (pair + 1) * LANES)
        q, k, v = q_ref[0, 0, :, cols], k_ref[0, 0, :, cols], v_ref[0, 0, :, cols]
        both = []
        for side in (low, ~low):
            s = dot(q * side.astype(BF), k, NT) * scale
            s = jnp.where(valid, s, -1e30)
            e = jnp.exp(s - jnp.max(s, axis=-1, keepdims=True))
            p = (e / jnp.sum(e, axis=-1, keepdims=True)).astype(BF)
            both.append(dot(p, v, NN))
        c_ref[0, :, cols] = jnp.where(low, both[0], both[1]).astype(BF)


def qkv_specs(rows, cols):
    return [pl.BlockSpec((1, 1, rows, cols), lambda i, *_, t=t: (t, i, 0, 0)) for t in range(3)]


def attend(text_len, qkv, scale):
    _, items, rows, cols = qkv.shape
    grid_spec = pltpu.PrefetchScalarGridSpec(
        num_scalar_prefetch=1,
        grid=(items,),
        in_specs=qkv_specs(rows, cols),
        out_specs=per_item((1, rows, cols)),
    )
    return pl.pallas_call(
        functools.partial(k_attend, scale=scale),
        grid_spec=grid_spec,
        out_shape=jax.ShapeDtypeStruct((items, rows, cols), BF),
        compiler_params=params(),
        cost_estimate=SHORT,
        name="attend",
    )(text_len, qkv, qkv, qkv)


def k_residual(tok_ref, cm_ref, cp_ref, wm_ref, wp_ref, vec_ref, h_ref, b_ref):
    y = dot(cm_ref[0], wm_ref[0], NT) + dot(cp_ref[0], wp_ref[0], NT)
    h = tok_ref[0].astype(F32) + (y + vec_ref[2:3, :])
    h_ref[0] = h
    hat, _ = normed(h)
    b_ref[0] = (hat * vec_ref[3:4, :] + vec_ref[4:5, :]).astype(BF)


def residual(tokens, mine, theirs, w_mine, w_theirs, vectors):
    items, rows, width = tokens.shape
    cols = mine.shape[2]
    return pl.pallas_call(
        k_residual,
        grid=(items,),
        in_specs=[
            per_item((1, rows, width)),
            per_item((1, rows, cols)),
            per_item((1, rows, cols)),
            full((1, width, cols)),
            full((1, width, cols)),
            full(vectors.shape),
        ],
        out_specs=[per_item((1, rows, width))] * 2,
        out_shape=[
            jax.ShapeDtypeStruct(tokens.shape, F32),
            jax.ShapeDtypeStruct(tokens.shape, BF),
        ],
        compiler_params=params(),
        cost_estimate=SHORT,
        name="residual",
    )(tokens, mine, theirs, w_mine, w_theirs, vectors)


def segments(rows):
    head = up_to(IMG, SUB)
    tail = IMG // SUB * SUB
    return (0, head), (tail, rows - tail), head


def segment_masks(rows):
    (a0, an), (b0, bn), _ = segments(rows)
    in_a = lax.broadcasted_iota(jnp.int32, (an, 1), 0) + a0 < IMG
    in_b = lax.broadcasted_iota(jnp.int32, (bn, 1), 0) + b0 >= IMG
    return in_a, in_b


def masked_parts(g_ref, i):
    rows = g_ref.shape[1]
    (a0, an), (b0, bn), _ = segments(rows)
    in_a, in_b = segment_masks(rows)
    g_a = jnp.where(in_a, g_ref[i, a0 : a0 + an, :].astype(F32), 0.0)
    g_b = jnp.where(in_b, g_ref[i, b0 : b0 + bn, :].astype(F32), 0.0)
    return g_a, g_b


def item_copies(refs, dest, sems):
    copies = []
    for ref in refs:
        if len(ref.shape) == 2:
            copies.append(
                pltpu.make_async_copy(ref, dest.at[len(copies)], sems.at[len(copies)])
            )
        else:
            for j in range(ref.shape[0]):
                copies.append(
                    pltpu.make_async_copy(ref.at[j], dest.at[len(copies)], sems.at[len(copies)])
                )
    return copies


def wait_item(copies, i):
    for n, c in enumerate(copies):

        @pl.when(i == n)
        def _(c=c):
            c.wait()


def write_chunks(slot_ref, base, acc, stage, outs, sems):
    count, _, rows, _ = stage.shape
    for c in range(count):
        stage[slot_ref[base + c]] = acc[:, c * rows : (c + 1) * rows, :].astype(BF)
    per = count // len(outs)
    copies = [
        pltpu.make_async_copy(stage.at[n * per : (n + 1) * per], out, sems.at[n])
        for n, out in enumerate(outs)
    ]
    run_copies(copies, start=True)
    run_copies(copies, wait=True)


def k_up(e_ref, off_ref, bias_ref, *rest, n_left):
    b_refs, pieces = rest[:n_left], rest[n_left:-6]
    act_ref, slope_ref, b_s, w_s, b_sem, w_sem = rest[-6:]
    i = pl.program_id(0)
    b_copies = item_copies(b_refs, b_s, b_sem)

    @pl.when(i == 0)
    def _():
        run_copies(b_copies[:1], start=True)
        w_copies = place_copies(off_ref, pieces, w_s, w_sem)
        run_copies(w_copies, start=True)
        run_copies(b_copies[1:], start=True)
        run_copies(w_copies, wait=True)

    wait_item(b_copies, i)
    seg_a, seg_b, _ = segments(b_s.shape[1])
    at = 0
    for which, (lo, n) in zip((0, 1), (seg_a, seg_b)):
        e = e_ref[which, i]
        u = dot(b_s[i, lo : lo + n, :], w_s[e], NN) + bias_ref[pl.ds(e, 1), :]
        cdf = 0.5 * (1.0 + lax.erf(u * ROOT_HALF))
        act_ref[0, at : at + n, :] = (u * cdf).astype(BF)
        slope_ref[0, at : at + n, :] = (cdf + u * jnp.exp(-0.5 * u * u) * INV_ROOT_TAU).astype(BF)
        at += n


def experts_up(experts, offsets, b, bias, pieces):
    items = experts.shape[1]
    rows, width = b[0].shape[-2:]
    e_count, _, hidden = pieces[0].shape[1:]
    count = len(pieces) * pieces[0].shape[0]
    (_, an), (_, bn), _ = segments(rows)
    grid_spec = pltpu.PrefetchScalarGridSpec(
        num_scalar_prefetch=2,
        grid=(items,),
        in_specs=[full((e_count, hidden))] + [ANY] * (len(b) + len(pieces)),
        out_specs=[per_item((1, an + bn, hidden))] * 2,
        scratch_shapes=[
            pltpu.VMEM((items, rows, width), BF),
            pltpu.VMEM((e_count, width, hidden), BF),
            pltpu.SemaphoreType.DMA((items,)),
            pltpu.SemaphoreType.DMA((count,)),
        ],
    )
    return pl.pallas_call(
        functools.partial(k_up, n_left=len(b)),
        grid_spec=grid_spec,
        out_shape=[jax.ShapeDtypeStruct((items, an + bn, hidden), BF)] * 2,
        compiler_params=params(),
        cost_estimate=SHORT,
        name="experts_up",
    )(experts, offsets, bias, *b, *pieces)


def k_weight_grad(e_ref, slot_ref, right_ref, *rest, n_left, n_out, base, own):
    lefts = rest[:n_left]
    outs = rest[n_left : n_left + n_out]
    left_s, dw_s, stage, left_sem, out_sem = rest[-5:]
    sums_ref = rest[n_left + n_out]
    i = pl.program_id(0)
    copies = item_copies(lefts, left_s, left_sem)

    @pl.when(i == 0)
    def _():
        run_copies(copies, start=True)
        dw_s[...] = jnp.zeros_like(dw_s)
        sums_ref[...] = jnp.zeros_like(sums_ref)

    wait_item(copies, i)
    at = 0
    for which, left in zip((0, 1), masked_parts(left_s, i)):
        e = e_ref[which, i]
        n = left.shape[0]
        dw_s[e] += dot(left.astype(BF), right_ref[0, at : at + n, :], TN)

        @pl.when(i < own)
        def _(left=left, e=e):
            sums_ref[pl.ds(e, 1), :] += jnp.sum(left, axis=0, keepdims=True)

        at += n

    @pl.when(i == pl.num_programs(0) - 1)
    def _():
        write_chunks(slot_ref, base, dw_s, stage, outs, out_sem)


def weight_grad(experts, slots, base, left, right, chunk, n_out, e_count, own):
    items, seg_rows, hidden = right.shape
    rows, width = left[0].shape[-2:]
    count = chunk[0] * n_out
    grid_spec = pltpu.PrefetchScalarGridSpec(
        num_scalar_prefetch=2,
        grid=(items,),
        in_specs=[per_item((1, seg_rows, hidden))] + [ANY] * len(left),
        out_specs=[ANY] * n_out + [full((e_count, width))],
        scratch_shapes=[
            pltpu.VMEM((items, rows, width), BF),
            pltpu.VMEM((e_count, width, hidden), F32),
            pltpu.VMEM((count,) + chunk[1:], BF),
            pltpu.SemaphoreType.DMA((items,)),
            pltpu.SemaphoreType.DMA((n_out,)),
        ],
    )
    return pl.pallas_call(
        functools.partial(
            k_weight_grad, n_left=len(left), n_out=n_out, base=base, own=own
        ),
        grid_spec=grid_spec,
        out_shape=[jax.ShapeDtypeStruct(chunk, BF)] * n_out
        + [jax.ShapeDtypeStruct((e_count, width), F32)],
        compiler_params=params(),
        cost_estimate=SHORT,
        name="weight_grad",
    )(experts, slots, right, *left)


def store_joined(ref, first, middle, second, tail, head):
    ref[0, :tail, :] = first[:tail].astype(BF)
    ref[0, tail:head, :] = middle.astype(BF)
    ref[0, head:, :] = second[head - tail :].astype(BF)


def k_back(e_ref, off_ref, slope_ref, *rest, n_left, n_up, own):
    g_s, w_up, w_down, sem_g, sem_up, sem_down = rest[-6:]
    do_ref, dp_ref, du_ref, gbu_ref = rest[-10:-6]
    lefts, ups, downs = rest[:n_left], rest[n_left : n_left + n_up], rest[n_left + n_up : -10]
    i = pl.program_id(0)
    copies = item_copies(lefts, g_s, sem_g)

    @pl.when(i == 0)
    def _():
        w_copies = place_copies(off_ref, downs, w_down, sem_down)
        run_copies(copies[:1] + w_copies, start=True)
        more = place_copies(off_ref, ups, w_up, sem_up)
        run_copies(more + copies[1:], start=True)
        gbu_ref[...] = jnp.zeros_like(gbu_ref)
        run_copies(w_copies + more, wait=True)

    wait_item(copies, i)
    rows = g_s.shape[1]
    seg_a, seg_b, head = segments(rows)
    tail = seg_b[0]
    at = 0
    both = []
    for which, g in zip((0, 1), masked_parts(g_s, i)):
        e = e_ref[which, i]
        n = g.shape[0]
        dact = dot(g.astype(BF), w_down[e], NN)
        du = (dact * slope_ref[0, at : at + n, :].astype(F32)).astype(BF)
        du_ref[0, at : at + n, :] = du
        gbu_ref[pl.ds(e, 1), :] += jnp.sum(du.astype(F32), axis=0, keepdims=True)
        both.append(dot(du, w_up[e], NT))
        at += n
    middle = both[0][tail:] + both[1][: head - tail]
    for cond, db_ref in ((i < own, do_ref), (i >= own, dp_ref)):

        @pl.when(cond)
        def _(db_ref=db_ref):
            store_joined(db_ref, both[0], middle, both[1], tail, head)


def own_and_other(rows, width, own):
    block = (1, rows, width)
    return [
        pl.BlockSpec(block, lambda i, *_: (jnp.minimum(i, own - 1), 0, 0)),
        pl.BlockSpec(block, lambda i, *_: (jnp.maximum(i - own, 0), 0, 0)),
    ]


def experts_back(experts, offsets, left, slope, ups, downs, own):
    rows, width = left[0].shape[-2:]
    e_count, _, hidden = ups[0].shape[1:]
    count = len(ups) * ups[0].shape[0]
    items, seg_rows, _ = slope.shape
    grid_spec = pltpu.PrefetchScalarGridSpec(
        num_scalar_prefetch=2,
        grid=(items,),
        in_specs=[per_item((1, seg_rows, hidden))]
        + [ANY] * (len(left) + len(ups) + len(downs)),
        out_specs=own_and_other(rows, width, own)
        + [per_item((1, seg_rows, hidden)), full((e_count, hidden))],
        scratch_shapes=[
            pltpu.VMEM((items, rows, width), BF),
            pltpu.VMEM((e_count, width, hidden), BF),
            pltpu.VMEM((e_count, width, hidden), BF),
            pltpu.SemaphoreType.DMA((items,)),
            pltpu.SemaphoreType.DMA((count,)),
            pltpu.SemaphoreType.DMA((count,)),
        ],
    )
    return pl.pallas_call(
        functools.partial(k_back, n_left=len(left), n_up=len(ups), own=own),
        grid_spec=grid_spec,
        out_shape=[
            jax.ShapeDtypeStruct((own, rows, width), BF),
            jax.ShapeDtypeStruct((items - own, rows, width), BF),
            jax.ShapeDtypeStruct((items, seg_rows, hidden), BF),
            jax.ShapeDtypeStruct((e_count, hidden), F32),
        ],
        compiler_params=params(),
        cost_estimate=SHORT,
        name="experts_back",
    )(experts, offsets, slope, *left, *ups, *downs)


def k_down(e_ref, off_ref, act_ref, *rest, own):
    zo_ref, zp_ref, w_down, sems = rest[-4:]
    pieces = rest[:-4]
    i = pl.program_id(0)

    @pl.when(i == 0)
    def _():
        copies = place_copies(off_ref, pieces, w_down, sems)
        run_copies(copies, start=True)
        run_copies(copies, wait=True)

    rows = zo_ref.shape[1]
    seg_a, seg_b, head = segments(rows)
    tail = seg_b[0]
    z_a = dot(act_ref[0, : seg_a[1], :], w_down[e_ref[0, i]], NT)
    z_b = dot(act_ref[0, seg_a[1] :, :], w_down[e_ref[1, i]], NT)
    image = lax.broadcasted_iota(jnp.int32, (head - tail, 1), 0) + tail < IMG
    middle = jnp.where(image, z_a[tail:], z_b[: head - tail])
    for cond, z_ref in ((i < own, zo_ref), (i >= own, zp_ref)):

        @pl.when(cond)
        def _(z_ref=z_ref):
            store_joined(z_ref, z_a, middle, z_b, tail, head)


def experts_down(experts, offsets, act, pieces, rows, own):
    items, seg_rows, hidden = act.shape
    e_count = pieces[0].shape[1]
    width = sum(p.shape[0] * p.shape[2] for p in pieces)
    count = len(pieces) * pieces[0].shape[0]
    grid_spec = pltpu.PrefetchScalarGridSpec(
        num_scalar_prefetch=2,
        grid=(items,),
        in_specs=[per_item((1, seg_rows, hidden))] + [ANY] * len(pieces),
        out_specs=own_and_other(rows, width, own),
        scratch_shapes=[
            pltpu.VMEM((e_count, width, hidden), BF),
            pltpu.SemaphoreType.DMA((count,)),
        ],
    )
    return pl.pallas_call(
        functools.partial(k_down, own=own),
        grid_spec=grid_spec,
        out_shape=[
            jax.ShapeDtypeStruct((own, rows, width), BF),
            jax.ShapeDtypeStruct((items - own, rows, width), BF),
        ],
        compiler_params=params(),
        cost_estimate=SHORT,
        name="experts_down",
    )(experts, offsets, act, *pieces)


def k_output(e_ref, h_ref, zm_ref, zp_ref, bias_ref, o_ref):
    i = pl.program_id(0)
    rows, keep = h_ref.shape[1], o_ref.shape[1]
    image = lax.broadcasted_iota(jnp.int32, (rows, 1), 0) < IMG
    bias = jnp.where(image, bias_ref[pl.ds(e_ref[0, i], 1), :], bias_ref[pl.ds(e_ref[1, i], 1), :])
    out = h_ref[0] + ((zm_ref[0].astype(F32) + zp_ref[0].astype(F32)) + bias)
    o_ref[0] = out[:keep].astype(BF)


def finish_output(experts, h, mine, theirs, bias, keep):
    items, rows, width = h.shape
    grid_spec = pltpu.PrefetchScalarGridSpec(
        num_scalar_prefetch=1,
        grid=(items,),
        in_specs=[per_item((1, rows, width))] * 3 + [full(bias.shape)],
        out_specs=per_item((1, keep, width)),
    )
    return pl.pallas_call(
        k_output,
        grid_spec=grid_spec,
        out_shape=jax.ShapeDtypeStruct((items, keep, width), BF),
        compiler_params=params(),
        cost_estimate=SHORT,
        name="finish_output",
    )(experts, h, mine, theirs, bias)


def k_attend_back(
    len_ref, dm_ref, dp_ref, h_ref, g_ref, tok_ref, q_ref, k_ref, v_ref, w_ref, wo_ref, vec_ref,
    dh_ref, dy_ref, dqkv_ref, da_ref, sums_ref, bias_ref, *, scale,
):
    rows, width = dh_ref.shape[1:]
    cols = q_ref.shape[3]
    i = pl.program_id(0)

    @pl.when(i == 0)
    def _():
        sums_ref[...] = jnp.zeros_like(sums_ref)
        bias_ref[...] = jnp.zeros_like(bias_ref)

    def add_rows(ref, at, value):
        ref[at : at + 1, :] += jnp.sum(value, axis=0, keepdims=True)

    db = dm_ref[0].astype(F32) + dp_ref[0].astype(F32)
    hat, spread = normed(h_ref[0])
    dh = g_ref[0].astype(F32) + norm_back(db, hat, spread, vec_ref[3:4, :])
    dh_ref[0] = dh
    dy = dh.astype(BF)
    dy_ref[0] = dy
    add_rows(sums_ref, 0, db * hat)
    add_rows(sums_ref, 1, db)
    add_rows(sums_ref, 2, dy.astype(F32))
    dctx = dot(dy, wo_ref[0], NN).astype(BF)
    valid = lax.broadcasted_iota(jnp.int32, (rows, 1), 0) < IMG + len_ref[i]
    low = lax.broadcasted_iota(jnp.int32, (1, LANES), 1) < HDIM
    for pair in range(cols // LANES):
        at = slice(pair * LANES, (pair + 1) * LANES)
        q, k, v = q_ref[0, 0, :, at], k_ref[0, 0, :, at], v_ref[0, 0, :, at]
        dc = dctx[:, at]
        parts = []
        for side in (low, ~low):
            only = side.astype(BF)
            s = dot(k * only, q, NT) * scale
            s = jnp.where(valid, s, -1e30)
            e = jnp.exp(s - jnp.max(s, axis=0, keepdims=True))
            p = e / jnp.sum(e, axis=0, keepdims=True)
            dp = dot(v * only, dc, NT)
            ds = (p * (dp - jnp.sum(p * dp, axis=0, keepdims=True))).astype(BF)
            parts.append((dot(ds, k, TN), dot(ds, q, NN), dot(p.astype(BF), dc, NN)))
        dqkv_ref[0, 0, :, at] = (jnp.where(low, parts[0][0], parts[1][0]) * scale).astype(BF)
        dqkv_ref[0, 1, :, at] = (jnp.where(low, parts[0][1], parts[1][1]) * scale).astype(BF)
        dqkv_ref[0, 2, :, at] = jnp.where(low, parts[0][2], parts[1][2]).astype(BF)
    da = dot(dqkv_ref[0, 0], w_ref[0], NT)
    da += dot(dqkv_ref[0, 1], w_ref[1], NT)
    da += dot(dqkv_ref[0, 2], w_ref[2], NT)
    add_rows(bias_ref, 0, dqkv_ref[0, 0].astype(F32))
    add_rows(bias_ref, 1, dqkv_ref[0, 2].astype(F32))
    hat, _ = normed(tok_ref[0].astype(F32))
    add_rows(sums_ref, 3, da * hat)
    add_rows(sums_ref, 4, da)
    da_ref[0] = da.astype(BF)


def attend_back(text_len, mine, theirs, h, g, tokens, qkv, weights, w_out, vectors, scale):
    items, rows, width = h.shape
    cols = qkv.shape[3]
    block = per_item((1, rows, width))
    grid_spec = pltpu.PrefetchScalarGridSpec(
        num_scalar_prefetch=1,
        grid=(items,),
        in_specs=[block] * 5
        + qkv_specs(rows, cols)
        + [full(weights.shape), full(w_out.shape), full(vectors.shape)],
        out_specs=[
            block,
            block,
            per_item((1, 3, rows, cols)),
            block,
            full((5, width)),
            full((2, cols)),
        ],
    )
    return pl.pallas_call(
        functools.partial(k_attend_back, scale=scale),
        grid_spec=grid_spec,
        out_shape=[
            jax.ShapeDtypeStruct((items, rows, width), F32),
            jax.ShapeDtypeStruct((items, rows, width), BF),
            jax.ShapeDtypeStruct((items, 3, rows, cols), BF),
            jax.ShapeDtypeStruct((items, rows, width), BF),
            jax.ShapeDtypeStruct((5, width), F32),
            jax.ShapeDtypeStruct((2, cols), F32),
        ],
        compiler_params=params(),
        cost_estimate=SHORT,
        name="attend_back",
    )(text_len, mine, theirs, h, g, tokens, qkv, qkv, qkv, weights, w_out, vectors)


def k_attn_grad(slot_ref, a_ref, d_ref, y_ref, c_ref, *rest, base):
    acc, stage, sems = rest[-3:]
    outs = rest[:-3]
    i = pl.program_id(0)

    @pl.when(i == 0)
    def _():
        acc[...] = jnp.zeros_like(acc)

    for t in range(4):
        left, right = (a_ref[0], d_ref[0, t]) if t < 3 else (y_ref[0], c_ref[0])
        acc[t] += dot(left, right, TN)

    @pl.when(i == pl.num_programs(0) - 1)
    def _():
        write_chunks(slot_ref, base, acc, stage, outs, sems)


def attn_grad(slots, base, a, dqkv, dy, ctx, chunk, n_out):
    items, rows, width = a.shape
    cols = ctx.shape[2]
    grid_spec = pltpu.PrefetchScalarGridSpec(
        num_scalar_prefetch=1,
        grid=(items,),
        in_specs=[
            per_item((1, rows, width)),
            per_item((1, 3, rows, cols)),
            per_item((1, rows, width)),
            per_item((1, rows, cols)),
        ],
        out_specs=[ANY] * n_out,
        scratch_shapes=[
            pltpu.VMEM((4, width, cols), F32),
            pltpu.VMEM((chunk[0] * n_out,) + chunk[1:], BF),
            pltpu.SemaphoreType.DMA((n_out,)),
        ],
    )
    return pl.pallas_call(
        functools.partial(k_attn_grad, base=base),
        grid_spec=grid_spec,
        out_shape=[jax.ShapeDtypeStruct(chunk, BF)] * n_out,
        compiler_params=params(),
        cost_estimate=SHORT,
        name="attn_grad",
    )(slots, a, dqkv, dy, ctx)


def k_token_grad(dh_ref, dm_ref, dp_ref, tok_ref, vec_ref, o_ref):
    keep = o_ref.shape[1]
    da = dm_ref[0].astype(F32) + dp_ref[0].astype(F32)
    hat, spread = normed(tok_ref[0].astype(F32))
    out = dh_ref[0] + norm_back(da, hat, spread, vec_ref[0:1, :])
    o_ref[0] = out[:keep]


def token_grad(dh, mine, theirs, tokens, vectors, keep):
    items, rows, width = dh.shape
    return pl.pallas_call(
        k_token_grad,
        grid=(items,),
        in_specs=[per_item((1, rows, width))] * 4 + [full(vectors.shape)],
        out_specs=per_item((1, keep, width)),
        out_shape=jax.ShapeDtypeStruct((items, keep, width), F32),
        compiler_params=params(),
        cost_estimate=SHORT,
        name="token_grad",
    )(dh, mine, theirs, tokens, vectors)


def swap(value, axis, size, mask):
    return lax.ppermute(value, axis, [(i, i ^ mask) for i in range(size)])


def tie(value, *others):
    return lax.optimization_barrier((value,) + others)[0]


def add_low(a, b):
    return (a.astype(F32) + b.astype(F32)).astype(BF)


def per_device(
    tokens, text_len, routes, attn_gain, attn_shift, w_qkv, b_qv, w_out, b_out, ffn_gain, ffn_shift,
    w_up, b_up, w_down, b_down, cotangent, *, dp, rep,
):
    items, seq, width = tokens.shape
    rows = up_to(seq, SUB)
    share = w_qkv.shape[1]
    cols = w_qkv.shape[2]
    hidden = w_up.shape[2] // 2
    e_count = w_up.shape[0]
    scale = 1.0 / math.sqrt(HDIM)
    me = lax.axis_index("dp")
    core = me % 2
    by_permute = dp == 16 and share % SUB == 0
    masks = [m for m in (1, 2, 4, 8, 16, 32, 64, 128) if m < dp]

    def peer(value):
        return lax.ppermute(value, "rep", [(i, i ^ 1) for i in range(rep)])

    def partner(value):
        return swap(value, "dp", dp, 1)

    def dp_swap(value, mask):
        return swap(value, "dp", dp, mask)

    def halves(w):
        mine = lax.dynamic_slice_in_dim(w, core * hidden, hidden, 2)
        other = lax.dynamic_slice_in_dim(w, (1 - core) * hidden, hidden, 2)
        return mine, other

    attn_shard = jnp.concatenate([w_qkv, w_out[None]], axis=0)
    vectors = jnp.stack([attn_gain, attn_shift, b_out, ffn_gain, ffn_shift])
    pad = ((0, 0), (0, rows - seq), (0, 0))
    tok = jnp.pad(tokens, pad)
    bias = jnp.stack([b_qv[0], jnp.zeros_like(b_qv[0]), b_qv[1]])
    experts = jnp.stack([routes[:, 0], routes[:, seq - 1]]).astype(jnp.int32)
    b_up_mine = lax.dynamic_slice_in_dim(b_up, core * hidden, hidden, 1)
    cot_partner = partner(cotangent)
    tok_tied = tie(tok, cot_partner)

    if by_permute:
        here = me.astype(jnp.int32)
        own_attn = attn_shard[None]
        z8a, z4a = dp_swap(own_attn, 8), dp_swap(own_attn, 4)
        za = [own_attn, z4a, z8a, dp_swap(z8a, 4)]
        xa = [dp_swap(p, 2) for p in za]
        attn_pieces = za + xa + [partner(p) for p in za + xa]
        rel = [0, 4, 8, 12]
        rel = rel + [r ^ 2 for r in rel]
        attn_off = (here ^ jnp.array(rel + [r ^ 1 for r in rel], jnp.int32)) * share
        rel = [r ^ j for r in rel for j in (0, 1)]
        ffn_off = (here ^ jnp.array(rel, jnp.int32)) * share
        mine, other = halves(w_up)
        up_own = jnp.stack([mine, partner(other)])
        mine, other = halves(w_down)
        down_own = jnp.stack([mine, partner(other)])
        ids = jnp.arange(dp, dtype=jnp.int32) ^ here
        slots = (
            (ids & 1) * (dp // 2)
            + (ids & 2) // 2 * (dp // 4)
            + (ids & 4) // 4 * (dp // 8)
            + (ids & 8) // 8
        )
        n_out = 4
        ffn_chunk, attn_chunk = (dp // 4, e_count, share, hidden), (dp // 4, 4, share, cols)

        up_own = tie(up_own, *za)
        z8u, z4u = dp_swap(up_own, 8), dp_swap(up_own, 4)
        x0u = dp_swap(tie(up_own, *xa), 2)
        x0d = dp_swap(tie(down_own, *xa), 2)
    else:
        attn_pieces = [lax.all_gather(attn_shard, "dp", axis=1, tiled=True)[None]]
        gathered = lax.all_gather(w_up, "dp", axis=1, tiled=True)
        up_pieces = [halves(gathered)[0][None]]
        gathered = lax.all_gather(w_down, "dp", axis=1, tiled=True)
        down_pieces = [halves(gathered)[0][None]]
        attn_off = ffn_off = slots = jnp.zeros((1,), jnp.int32)
        n_out = 1
        ffn_chunk, attn_chunk = (1, e_count, width, hidden), (1, 4, width, cols)

    a, qkv, attn_w, out_w = project(tok_tied, vectors, bias, attn_pieces, attn_off)
    half = width // 2
    out_mine = lax.dynamic_slice_in_dim(out_w, core * half, half, 1)
    stage = [out_w]
    if by_permute:
        stage = stage + [z4u, z8u, x0u, x0d]
        z12u = dp_swap(tie(z8u, *stage), 4)
        x1u = dp_swap(tie(z4u, *stage), 2)
    out_half = peer(tie(out_mine, *stage))
    experts_partner = partner(tie(experts, *stage))
    ctx = attend(tie(text_len, *stage), qkv, scale)
    stage = [ctx, out_half, experts_partner]
    if by_permute:
        stage = stage + [z12u, x1u]
        x2u = dp_swap(tie(z8u, *stage), 2)
        x3u = dp_swap(tie(z12u, *stage), 2)
        z8d, z4d = (dp_swap(tie(down_own, *stage), r) for r in (8, 4))
    ctx_theirs = peer(tie(ctx, *stage))
    out_other = partner(tie(out_half, *stage))
    out_theirs = jnp.where(
        core == 0,
        jnp.concatenate([out_half, out_other], axis=1),
        jnp.concatenate([out_other, out_half], axis=1),
    )
    cots = [jnp.pad(tie(v, *stage), pad) for v in (cotangent, cot_partner)]
    experts_two = jnp.concatenate([experts, experts_partner], axis=1)
    stage = [*cots, ctx]
    if by_permute:
        stage = stage + [x2u]
    h, b = residual(tok, ctx, ctx_theirs, out_w, out_theirs, tie(vectors, *stage))
    stage = [h]
    if by_permute:
        stage = stage + [x3u, z8d, z4d]
        x1d = dp_swap(tie(z4d, *stage), 2)
        x2d = dp_swap(tie(z8d, *stage), 2)
        z12d = dp_swap(tie(z8d, *stage), 4)
        up_pieces = [up_own, z4u, z8u, z12u, x0u, x1u, x2u, x3u]
    b_two = [b, partner(tie(b, *stage))]

    act, slope = experts_up(tie(experts_two, *stage), ffn_off, b_two, b_up_mine, up_pieces)
    stage = [act]
    if by_permute:
        stage = stage + [x1d, z12d, x2d]
        x3d = dp_swap(tie(z12d, *stage), 2)
    *down_grad, grad_b_down = weight_grad(
        tie(experts_two, *stage), slots, 0, cots, act, ffn_chunk, n_out, e_count, items
    )
    stage = [grad_b_down]
    if by_permute:
        down_pieces = [down_own, z4d, z8d, z12d, x0d, x1d, x2d, x3d]

        def near(parts, core_slot, *others):
            return dp_swap(tie(parts[2 * core_slot + 1], *others), 2)

        def middle(parts, core_slot, got, *others):
            keep, got = tie(parts[2 * core_slot], got, *others), tie(got, *others)
            both = keep[2:4].astype(F32) + got[2:4].astype(F32)
            return keep, got, dp_swap(both.astype(BF), 4)

        def last(state, *others):
            keep, got, mid = state
            mid = tie(mid, *others)
            part = keep[1].astype(F32) + got[1].astype(F32) + mid[1].astype(F32)
            return keep, got, mid, dp_swap(part.astype(BF), 8)

        def total(state):
            keep, got, mid, end = state
            return (
                keep[0].astype(F32)
                + got[0].astype(F32)
                + mid[0].astype(F32)
                + end.astype(F32)
            )

        stage = stage + [x3d]
        dn1 = near(down_grad, 1, *stage)
    db_own, db_other, du, grad_b_up = experts_back(
        tie(experts_two, *stage), ffn_off, cots, slope, up_pieces, down_pieces, items
    )
    db = add_low(db_own, partner(db_other))
    stage = [db]
    if by_permute:
        stage = stage + [dn1]
        dm1 = middle(down_grad, 1, dn1, *stage)
        dn0 = near(down_grad, 0, *stage)
    db_theirs = peer(tie(db, *stage))
    *up_grad, _ = weight_grad(
        tie(experts_two, *stage), slots, 0, b_two, du, ffn_chunk, n_out, e_count, 0
    )
    stage = [up_grad[0]]
    if by_permute:
        stage = stage + [dm1[2]]
        un1 = near(up_grad, 1, *stage)
        de1 = last(dm1, *stage)
    z_own, z_other = experts_down(
        tie(experts_two, *stage), ffn_off, act, down_pieces, rows, items
    )
    stage = [z_own, db_theirs]
    if by_permute:
        stage = stage + [dn0, de1[3]]
        dm0 = middle(down_grad, 0, dn0, *stage)
        un0 = near(up_grad, 0, *stage)
    z = add_low(z_own, partner(tie(z_other, *stage)))
    z_theirs = peer(z)

    dh, dy, dqkv, da, sums, bias_sums = attend_back(
        tie(text_len, z), db, db_theirs, h, cots[0], tok, qkv, attn_w, out_w, vectors, scale
    )
    stage = [bias_sums, z_theirs]
    if by_permute:
        stage = stage + [dm0[2], un1]
        um1 = middle(up_grad, 1, un1, *stage)
        de0 = last(dm0, *stage)
    da_theirs = peer(tie(da, *stage))
    first_norm = tie(sums[3:5], *stage)
    first_norm_theirs = peer(first_norm)
    attn_parts = attn_grad(tie(slots, *stage), 0, a, dqkv, dy, ctx, attn_chunk, n_out)

    stage = [attn_parts[0], first_norm_theirs]
    up_pair = jnp.zeros((2, e_count, hidden), F32)
    up_pair = lax.dynamic_update_slice_in_dim(up_pair, grad_b_up[None], core, 0)
    small = jnp.concatenate(
        [
            (first_norm + first_norm_theirs).reshape(-1),
            sums[0:3].reshape(-1),
            grad_b_down.reshape(-1),
            up_pair.reshape(-1),
            bias_sums.reshape(-1),
        ]
    ).reshape(-1, LANES)
    steps = list(masks)

    def add_step(*others):
        nonlocal small
        small = tie(small, *others)
        got = swap(small, "dp", dp, steps.pop(0))
        small = small + got
        return got

    if by_permute:
        send = add_low(attn_parts[1], partner(attn_parts[3]))
        keep = add_low(attn_parts[0], partner(attn_parts[2]))
        stage = stage + [um1[2], de0[3], un0]
        an = near([keep, send], 0, *stage)
        ue1 = last(um1, *stage)
        um0 = middle(up_grad, 0, un0, *stage)
        down_other = total(tie(de1, *stage))
        down_got = partner(down_other)
    got = add_step(*stage)
    output = finish_output(tie(experts, *stage), h, z, z_theirs, b_down, seq)
    stage = [output, got]
    if by_permute:
        stage = stage + [down_got]
        down_mine = total(tie(de0, *stage))
    got = add_step(*stage)
    grad_tokens = token_grad(dh, da, da_theirs, tok, tie(vectors, *stage), seq)
    stage = [grad_tokens, got]
    if by_permute:
        stage = stage + [um0[2], ue1[3]]
        ue0 = last(um0, *stage)
        up_other = total(tie(ue1, *stage))
        up_got = partner(up_other)
    got = add_step(*stage)

    if by_permute:

        def joined(own, got):
            whole = jnp.zeros((e_count, share, 2 * hidden), F32)
            whole = lax.dynamic_update_slice_in_dim(whole, got, (1 - core) * hidden, 2)
            return lax.dynamic_update_slice_in_dim(whole, own, core * hidden, 2)

        am = middle([keep, send], 0, an, up_other)
        grad_w_down = joined(tie(down_mine, am[0]), down_got)
        ae = last(am, grad_w_down)
        grad_w_up = joined(total(ue0), up_got)
        grad_attn = total(tie(ae, grad_w_up))
        grad_w_qkv, grad_w_out = grad_attn[:3], grad_attn[3]
    else:

        def finish(chunk):
            whole = jnp.zeros((e_count, width, 2 * hidden), BF)
            whole = lax.dynamic_update_slice_in_dim(whole, chunk[0], core * hidden, 2)
            return lax.psum_scatter(whole, "dp", scatter_dimension=1, tiled=True).astype(F32)

        grad_w_down, grad_w_up = finish(down_grad[0]), finish(up_grad[0])
        grad_attn = lax.psum_scatter(attn_parts[0][0], "dp", scatter_dimension=1, tiled=True)
        grad_w_qkv, grad_w_out = grad_attn[:3].astype(F32), grad_attn[3].astype(F32)

    while steps:
        add_step()
    small = small.reshape(-1)
    at = 0

    def take(*shape):
        nonlocal at
        n = math.prod(shape)
        piece = small[at : at + n].reshape(shape)
        at += n
        return piece

    norm_one, norm_two, grad_b_out = take(2, width), take(2, width), take(width)
    total_down = take(e_count, width)
    total_up = jnp.moveaxis(take(2, e_count, hidden), 0, 1).reshape(e_count, 2 * hidden)
    total_qv = take(2, cols)
    return (
        output,
        grad_tokens,
        grad_w_qkv,
        grad_w_out,
        grad_w_up,
        grad_w_down,
        total_qv,
        grad_b_out,
        total_up,
        total_down,
        jnp.concatenate([norm_one, norm_two], axis=0),
    )


def solution(mesh):
    body = functools.partial(per_device, dp=mesh.shape["dp"], rep=mesh.shape["rep"])
    return jax.shard_map(
        body,
        mesh=mesh,
        in_specs=(
            P("dp", None, None),
            P("dp"),
            P("dp", None),
            P(),
            P(),
            P(None, "dp", "rep"),
            P(None, "rep"),
            P("dp", "rep"),
            P(),
            P(),
            P(),
            P(None, "dp", "rep"),
            P(None, "rep"),
            P(None, "dp", "rep"),
            P(),
            P("dp", None, None),
        ),
        out_specs=(
            P("dp", None, None),
            P("dp", None, None),
            P(None, "dp", "rep"),
            P("dp", "rep"),
            P(None, "dp", "rep"),
            P(None, "dp", "rep"),
            P(None, "rep"),
            P(),
            P(None, "rep"),
            P(),
            P(),
        ),
        check_vma=False,
    )
```

profile of v0, /device:TPU:0, one launch (start us, length us, event | category | flops | bytes accessed | tf_op | source)
XLA Modules:
  0.0 327.0 jit_solution(12841316130278769815)
XLA Ops:
  2.2 3.8 %collective-permute-start.2 = (bf16[1,4,48,384]{3,2,1,0:T(8,128)(2,1)S(1)}, bf16[1,4,48,384]{3,2,1,0:T(8,128)(2,1)S(1)}, u32[]{:S(2)}, u32[]{:S(2)}) collective-permute-start(bf16[1,4,48,384]{3,2,1,0:T(8,128)(2,1)S(1)} %maximum_bitcast_fusion.rest_0_), channel_id=1, source_target_pairs={{0,16},{2,18},{4,20},{6,22},{8,24},{10,26},{12,28},{14,30},{16,0},... | collective-permute-start | bytes 442376 | tf_op jit(solution)/shard_map/ppermute | solution.py:731
  10.3 3.4 %collective-permute-done.2.rest_2_ = bf16[1,4,48,384]{3,2,1,0:T(8,128)(2,1)S(1)} collective-permute-done((bf16[1,4,48,384]{3,2,1,0:T(8,128)(2,1)S(1)}, bf16[1,4,48,384]{3,2,1,0:T(8,128)(2,1)S(1)}, u32[]{:S(2)}, u32[]{:S(2)}) %collective-permute-start.2) | collective-permute-done | bytes 147488 | tf_op jit(solution)/shard_map/ppermute | solution.py:731
  36.2 8.8 %project.1 = (bf16[3,272,768]{2,1,0:T(8,128)(2,1)}, bf16[3,3,272,384]{3,2,1,0:T(8,128)(2,1)}, bf16[3,768,384]{2,1,0:T(8,128)(2,1)}, bf16[1,768,384]{2,1,0:T(8,128)(2,1)}) custom-call(s32[16]{0:T(128)} %xor_multiply_fusion.1.off_ref, bf16[3,272,768]{2,1,0:T(8,128)(2,1)} %pad.10.tok_ref, f32[5,768]{1,0:T(8,128)} %stack.48.vec_ref, ...), custom_call_target="tpu_custom_call" | custom-call | flops 1 | bytes 1 | tf_op jit(solution)/shard_map/project/pallas_call | solution.py:138
  45.0 5.6 %collective-permute-done.17.rest_3_ = bf16[2,3,48,768]{3,2,1,0:T(8,128)(2,1)S(1)} collective-permute-done((bf16[2,3,48,768]{3,2,1,0:T(8,128)(2,1)S(1)}, bf16[2,3,48,768]{3,2,1,0:T(8,128)(2,1)S(1)}, u32[]{:S(2)}, u32[]{:S(2)}) %collective-permute-start.17) | collective-permute-done | bytes 442400 | tf_op jit(solution)/shard_map/ppermute | solution.py:731
  59.0 8.3 %attend.1.cm_ref.c_ref = bf16[3,272,384]{2,1,0:T(8,128)(2,1)} custom-call(s32[3]{0:T(128)} %len_ref.1, bf16[3,3,272,384]{3,2,1,0:T(8,128)(2,1)} %get-tuple-element.125.q_ref.k_ref.v_ref, bf16[3,3,272,384]{3,2,1,0:T(8,128)(2,1)} %get-tuple-element.125.q_ref.k_ref.v_ref, bf16[3,3,272,384]{3,2,1,0:T(8,128)(2,1)} %get-tuple-element.125.q_ref.k_ref.v_ref), custom_call_target="tpu_custom_call" | custom-call | flops 1 | bytes 1 | tf_op jit(solution)/shard_map/attend/pallas_call | solution.py:183
  78.1 3.4 %collective-permute-done.28.rest_8_ = bf16[2,3,48,768]{3,2,1,0:T(8,128)(2,1)S(1)} collective-permute-done((bf16[2,3,48,768]{3,2,1,0:T(8,128)(2,1)S(1)}, bf16[2,3,48,768]{3,2,1,0:T(8,128)(2,1)S(1)}, u32[]{:S(2)}, u32[]{:S(2)}) %collective-permute-start.28) | collective-permute-done | bytes 442400 | tf_op jit(solution)/shard_map/ppermute | solution.py:731
  81.5 2.9 collective-permute-done.26.cp_ref
  84.4 5.5 %residual.1 = (f32[3,272,768]{2,1,0:T(8,128)}, bf16[3,272,768]{2,1,0:T(8,128)(2,1)}) custom-call(bf16[3,272,768]{2,1,0:T(8,128)(2,1)} %pad.10.tok_ref, bf16[3,272,384]{2,1,0:T(8,128)(2,1)} %attend.1.cm_ref.c_ref, bf16[3,272,384]{2,1,0:T(8,128)(2,1)} %collective-permute-done.26.cp_ref, bf16[1,768,384]{2,1,0:T(8,128)(2,1)} %get-tuple-element.119.wm_ref.wo_ref, ...), custom_call_target="tpu_custom_call" | custom-call | flops 1 | bytes 1 | tf_op jit(solution)/shard_map/residual/pallas_call | solution.py:204
  97.5 10.2 %experts_up.1 = (bf16[6,288,768]{2,1,0:T(8,128)(2,1)}, bf16[6,288,768]{2,1,0:T(8,128)(2,1)}) custom-call(s32[2,6]{1,0:T(2,128)} %pad_add_fusion.1.e_ref, s32[16]{0:T(128)} %xor_multiply_fusion.off_ref, f32[3,768]{1,0:T(4,128)} %constant_dynamic-slice_fusion.bias_ref, bf16[3,272,768]{2,1,0:T(8,128)(2,1)} %get-tuple-element.140.rest_0_, ...), custom_call_target="tpu_custom_call" | custom-call | flops 1 | bytes 1 | tf_op jit(solution)/shard_map/experts_up/pallas_call | solution.py:328
  107.7 6.7 %collective-permute-done.33.rest_5_ = bf16[2,3,48,768]{3,2,1,0:T(8,128)(2,1)S(1)} collective-permute-done((bf16[2,3,48,768]{3,2,1,0:T(8,128)(2,1)}, bf16[2,3,48,768]{3,2,1,0:T(8,128)(2,1)S(1)}, u32[]{:S(2)}, u32[]{:S(2)}) %collective-permute-start.33) | collective-permute-done | bytes 442400 | tf_op jit(solution)/shard_map/ppermute | solution.py:731
  115.8 13.3 %weight_grad.2 = (bf16[4,3,48,768]{3,2,1,0:T(8,128)(2,1)}, bf16[4,3,48,768]{3,2,1,0:T(8,128)(2,1)}, bf16[4,3,48,768]{3,2,1,0:T(8,128)(2,1)}, bf16[4,3,48,768]{3,2,1,0:T(8,128)(2,1)}, f32[3,768]{1,0:T(4,128)}) custom-call(s32[2,6]{1,0:T(2,128)} %pad_add_fusion.1.e_ref, s32[16]{0:T(128)} %fusion.6.slot_ref, ...), custom_call_target="tpu_custom_call" | custom-call | flops 1 | bytes 1 | tf_op jit(solution)/shard_map/weight_grad/pallas_call | solution.py:387
  129.2 15.0 %experts_back.1 = (f32[2,3,768]{2,1,0:T(4,128)S(1)}, bf16[3,272,768]{2,1,0:T(8,128)(2,1)S(1)}, bf16[3,272,768]{2,1,0:T(8,128)(2,1)}, bf16[6,288,768]{2,1,0:T(8,128)(2,1)}) fusion(f32[2,3,768]{2,1,0:T(4,128)S(1)} %broadcast_in_dim.14, s32[]{:T(128)S(6)} %select_n.54, s32[2,6]{1,0:T(2,128)S(1)} %copy-done.55, s32[16]{0:T(128)S(1)} %copy-done.57, ...), kind=kCustom, calls=%fused_computation.33 | custom fusion | bytes 17413636 | tf_op jit(solution)/shard_map/experts_back/pallas_call | solution.py:474
  147.8 18.8 %collective-permute-done.38 = bf16[4,3,48,768]{3,2,1,0:T(8,128)(2,1)S(1)} collective-permute-done((bf16[4,3,48,768]{3,2,1,0:T(8,128)(2,1)}, bf16[4,3,48,768]{3,2,1,0:T(8,128)(2,1)S(1)}, u32[]{:S(2)}, u32[]{:S(2)}) %collective-permute-start.38) | collective-permute-done | bytes 884768 | tf_op jit(solution)/shard_map/ppermute | solution.py:731
  172.0 13.2 %weight_grad.3 = (bf16[4,3,48,768]{3,2,1,0:T(8,128)(2,1)}, bf16[4,3,48,768]{3,2,1,0:T(8,128)(2,1)}, bf16[4,3,48,768]{3,2,1,0:T(8,128)(2,1)}, bf16[4,3,48,768]{3,2,1,0:T(8,128)(2,1)}, f32[3,768]{1,0:T(4,128)}) custom-call(s32[2,6]{1,0:T(2,128)} %pad_add_fusion.1.e_ref, s32[16]{0:T(128)} %fusion.6.slot_ref, bf16[6,288,768]{2,1,0:T(8,128)(2,1)} %get-tuple-element.231.right_ref, ...), custom_call_target="tpu_custom_call" | custom-call | flops 1 | bytes 1 | tf_op jit(solution)/shard_map/weight_grad/pallas_call | solution.py:387
  187.4 10.8 %experts_down.1 = (bf16[3,272,768]{2,1,0:T(8,128)(2,1)}, bf16[3,272,768]{2,1,0:T(8,128)(2,1)}) custom-call(s32[2,6]{1,0:T(2,128)} %pad_add_fusion.1.e_ref, s32[16]{0:T(128)} %xor_multiply_fusion.off_ref, bf16[6,288,768]{2,1,0:T(8,128)(2,1)} %get-tuple-element.141.right_ref.act_ref, bf16[2,3,48,768]{3,2,1,0:T(8,128)(2,1)} %copy-done.8, ...), custom_call_target="tpu_custom_call" | custom-call | flops 1 | bytes 1 | tf_op jit(solution)/shard_map/experts_down/pallas_call | solution.py:529
  200.0 3.1 collective-permute-done.43
  209.3 20.4 %attend_back.1 = (f32[3,272,768]{2,1,0:T(8,128)}, bf16[3,272,768]{2,1,0:T(8,128)(2,1)}, bf16[3,3,272,384]{3,2,1,0:T(8,128)(2,1)}, bf16[3,272,768]{2,1,0:T(8,128)...) custom-call(s32[3]{0:T(128)} %len_ref.1, bf16[3,272,768]{2,1,0:T(8,128)(2,1)} %copy-done.6, bf16[3,272,768]{2,1,0:T(8,128)(2,1)} %copy-done.22, ...), custom_call_target="tpu_custom_call" | custom-call | flops 1 | bytes 1 | tf_op jit(solution)/shard_map/attend_back/pallas_call | solution.py:644
  242.0 9.1 %attn_grad.1 = (bf16[4,4,48,384]{3,2,1,0:T(8,128)(2,1)}, bf16[4,4,48,384]{3,2,1,0:T(8,128)(2,1)}, bf16[4,4,48,384]{3,2,1,0:T(8,128)(2,1)}, bf16[4,4,48,384]{3,2,1,0:T(8,128)(2,1)}) custom-call(s32[16]{0:T(128)} %fusion.6.slot_ref, bf16[3,272,768]{2,1,0:T(8,128)(2,1)} %get-tuple-element.176.a_ref, bf16[3,3,272,384]{3,2,1,0:T(8,128)(2,1)} %get-tuple-element.177.d_ref, ...), custom_call_target="tpu_custom_call" | custom-call | flops 1 | bytes 1 | tf_op jit(solution)/shard_map/attn_grad/pallas_call | solution.py:698
  251.9 3.5 %collective-permute-done.48 = bf16[2,3,48,768]{3,2,1,0:T(8,128)(2,1)S(1)} collective-permute-done((bf16[2,3,48,768]{3,2,1,0:T(8,128)(2,1)}, bf16[2,3,48,768]{3,2,1,0:T(8,128)(2,1)S(1)}, u32[]{:S(2)}, u32[]{:S(2)}) %collective-permute-start.48) | collective-permute-done | bytes 442400 | tf_op jit(solution)/shard_map/ppermute | solution.py:731
  261.7 5.2 %finish_output.1 = bf16[3,261,768]{2,1,0:T(8,128)(2,1)} custom-call(s32[2,3]{1,0:T(2,128)} %copy-done.63, f32[3,272,768]{2,1,0:T(8,128)} %get-tuple-element.135.h_ref, bf16[3,272,768]{2,1,0:T(8,128)(2,1)} %copy-done.4, bf16[3,272,768]{2,1,0:T(8,128)(2,1)} %collective-permute-done.44.zp_ref, f32[3,768]{1,0:T(4,128)} %bias_ref.1), custom_call_target="tpu_custom_call" | custom-call | flops 1 | bytes 1 | tf_op jit(solution)/shard_map/finish_output/pallas_call | solution.py:559
  276.2 10.2 %collective-permute-done.58 = f32[90,128]{1,0:T(8,128)S(1)} collective-permute-done((f32[90,128]{1,0:T(8,128)S(1)}, f32[90,128]{1,0:T(8,128)S(1)}, u32[]{:S(2)}, u32[]{:S(2)}) %collective-permute-start.58) | collective-permute-done | bytes 46112 | tf_op jit(solution)/shard_map/ppermute | solution.py:731
  286.4 5.7 %token_grad.1 = f32[3,261,768]{2,1,0:T(8,128)} custom-call(f32[3,272,768]{2,1,0:T(8,128)} %get-tuple-element.189.dh_ref, bf16[3,272,768]{2,1,0:T(8,128)(2,1)} %get-tuple-element.191.dm_ref, bf16[3,272,768]{2,1,0:T(8,128)(2,1)} %collective-permute-done.51.dp_ref, bf16[3,272,768]{2,1,0:T(8,128)(2,1)} %pad.10.tok_ref, f32[5,768]{1,0:T(8,128)} %stack.48.vec_ref), custom_call_target="tpu_custom_call" | custom-call | flops 1 | bytes 1 | tf_op jit(solution)/shard_map/token_grad/pallas_call | solution.py:718
  301.6 7.2 %collective-permute-done.65 = f32[90,128]{1,0:T(8,128)S(1)} collective-permute-done((f32[90,128]{1,0:T(8,128)S(1)}, f32[90,128]{1,0:T(8,128)S(1)}, u32[]{:S(2)}, u32[]{:S(2)}) %collective-permute-start.65) | collective-permute-done | bytes 46112 | tf_op jit(solution)/shard_map/ppermute | solution.py:731
  318.9 5.7 %collective-permute-done.61 = bf16[4,48,384]{2,1,0:T(8,128)(2,1)S(1)} collective-permute-done((bf16[4,48,384]{2,1,0:T(8,128)(2,1)S(1)}, bf16[4,48,384]{2,1,0:T(8,128)(2,1)S(1)}, u32[]{:S(2)}, u32[]{:S(2)}) %collective-permute-start.61) | collective-permute-done | bytes 147488 | tf_op jit(solution)/shard_map/ppermute | solution.py:731
  (337 shorter events, 125.5 us)
Async XLA Ops:
  0.7 33.4 %collective-permute-start = (bf16[3,261,768]{2,1,0:T(8,128)(2,1)}, bf16[3,261,768]{2,1,0:T(8,128)(2,1)}, u32[]{:S(2)}, u32[]{:S(2)}) collective-permute-start(bf16[3,261,768]{2,1,0:T(8,128)(2,1)} %param.33), channel_id=1, source_target_pairs={{0,2},{2,0},{4,6},{6,4},{8,10},{10,8},{12,14},{14,12},{16,18},{18,... | collective-permute-start | bytes 3608072 | tf_op jit(solution)/shard_map/ppermute | solution.py:731
  28.5 22.1 %collective-permute-start.17 = (bf16[2,3,48,768]{3,2,1,0:T(8,128)(2,1)S(1)}, bf16[2,3,48,768]{3,2,1,0:T(8,128)(2,1)S(1)}, u32[]{:S(2)}, u32[]{:S(2)}) collective-permute-start(bf16[2,3,48,768]{3,2,1,0:T(8,128)(2,1)S(1)} %pad_maximum_fusion.rest_2_), channel_id=1, source_target_pairs={{0,8},{2,10},{4,12},{6,14},{8,0},{10,2},{12,4},{14,6},{16,24},{18,... | collective-permute-start | bytes 1327112 | tf_op jit(solution)/shard_map/ppermute | solution.py:731
  29.4 21.2 %collective-permute-start.18 = (bf16[2,3,48,768]{3,2,1,0:T(8,128)(2,1)S(1)}, bf16[2,3,48,768]{3,2,1,0:T(8,128)(2,1)S(1)}, u32[]{:S(2)}, u32[]{:S(2)}) collective-permute-start(bf16[2,3,48,768]{3,2,1,0:T(8,128)(2,1)S(1)} %pad_maximum_fusion.rest_2_), channel_id=1, source_target_pairs={{0,16},{2,18},{4,20},{6,22},{8,24},{10,26},{12,28},{14,30},{16,0},... | collective-permute-start | bytes 1327112 | tf_op jit(solution)/shard_map/ppermute | solution.py:731
  31.4 19.2 %collective-permute-start.19 = (bf16[2,3,48,768]{3,2,1,0:T(8,128)(2,1)S(1)}, bf16[2,3,48,768]{3,2,1,0:T(8,128)(2,1)S(1)}, u32[]{:S(2)}, u32[]{:S(2)}) collective-permute-start(bf16[2,3,48,768]{3,2,1,0:T(8,128)(2,1)S(1)} %pad_maximum_fusion.rest_2_), channel_id=1, source_target_pairs={{0,4},{2,6},{4,0},{6,2},{8,12},{10,14},{12,8},{14,10},{16,20},{18,... | collective-permute-start | bytes 1327112 | tf_op jit(solution)/shard_map/ppermute | solution.py:731
  32.3 20.9 %collective-permute-start.21 = (bf16[2,3,48,768]{3,2,1,0:T(8,128)(2,1)S(1)}, bf16[2,3,48,768]{3,2,1,0:T(8,128)(2,1)S(1)}, u32[]{:S(2)}, u32[]{:S(2)}) collective-permute-start(bf16[2,3,48,768]{3,2,1,0:T(8,128)(2,1)S(1)} %pad_maximum_fusion.1.rest_0_), channel_id=1, source_target_pairs={{0,4},{2,6},{4,0},{6,2},{8,12},{10,14},{12,8},{14,10},{16,20},{18,... | collective-permute-start | bytes 1327112 | tf_op jit(solution)/shard_map/ppermute | solution.py:731
  70.0 22.0 %collective-permute-start.30 = (bf16[2,3,48,768]{3,2,1,0:T(8,128)(2,1)S(1)}, bf16[2,3,48,768]{3,2,1,0:T(8,128)(2,1)S(1)}, u32[]{:S(2)}, u32[]{:S(2)}) collective-permute-start(bf16[2,3,48,768]{3,2,1,0:T(8,128)(2,1)S(1)} %pad_maximum_fusion.1.rest_0_), channel_id=1, source_target_pairs={{0,16},{2,18},{4,20},{6,22},{8,24},{10,26},{12,28},{14,30},{16,0},... | collective-permute-start | bytes 1327112 | tf_op jit(solution)/shard_map/ppermute | solution.py:731
  71.4 20.9 %collective-permute-start.31 = (bf16[2,3,48,768]{3,2,1,0:T(8,128)(2,1)S(1)}, bf16[2,3,48,768]{3,2,1,0:T(8,128)(2,1)}, u32[]{:S(2)}, u32[]{:S(2)}) collective-permute-start(bf16[2,3,48,768]{3,2,1,0:T(8,128)(2,1)S(1)} %pad_maximum_fusion.1.rest_0_), channel_id=1, source_target_pairs={{0,8},{2,10},{4,12},{6,14},{8,0},{10,2},{12,4},{14,6},{16,24},{18,... | collective-permute-start | bytes 1327112 | tf_op jit(solution)/shard_map/ppermute | solution.py:731
  71.7 20.5 %collective-permute-start.29 = (bf16[2,3,48,768]{3,2,1,0:T(8,128)(2,1)S(1)}, bf16[2,3,48,768]{3,2,1,0:T(8,128)(2,1)S(1)}, u32[]{:S(2)}, u32[]{:S(2)}) collective-permute-start(bf16[2,3,48,768]{3,2,1,0:T(8,128)(2,1)S(1)} %collective-permute-done.24.rest_5_), channel_id=1, source_target_pairs={{0,4},{2,6},{4,0},{6,2},{8,12},{10,14},{12,8},{14,10},{16,20},{18,... | collective-permute-start | bytes 1327112 | tf_op jit(solution)/shard_map/ppermute | solution.py:731
  93.2 21.2 %collective-permute-start.33 = (bf16[2,3,48,768]{3,2,1,0:T(8,128)(2,1)}, bf16[2,3,48,768]{3,2,1,0:T(8,128)(2,1)S(1)}, u32[]{:S(2)}, u32[]{:S(2)}) collective-permute-start(bf16[2,3,48,768]{3,2,1,0:T(8,128)(2,1)} %collective-permute-done.31.rest_1_), channel_id=1, source_target_pairs={{0,4},{2,6},{4,0},{6,2},{8,12},{10,14},{12,8},{14,10},{16,20},{18,... | collective-permute-start | bytes 1327112 | tf_op jit(solution)/shard_map/ppermute | solution.py:731
  144.3 22.3 %collective-permute-start.38 = (bf16[4,3,48,768]{3,2,1,0:T(8,128)(2,1)}, bf16[4,3,48,768]{3,2,1,0:T(8,128)(2,1)S(1)}, u32[]{:S(2)}, u32[]{:S(2)}) collective-permute-start(bf16[4,3,48,768]{3,2,1,0:T(8,128)(2,1)} %get-tuple-element.152), channel_id=1, source_target_pairs={{0,4},{2,6},{4,0},{6,2},{8,12},{10,14},{12,8},{14,10},{16,20},{18,... | collective-permute-start | bytes 2654216 | tf_op jit(solution)/shard_map/ppermute | solution.py:731
  166.6 32.4 %collective-permute-start.40 = (bf16[3,272,768]{2,1,0:T(8,128)(2,1)S(1)}, bf16[3,272,768]{2,1,0:T(8,128)(2,1)S(1)}, u32[]{:S(2)}, u32[]{:S(2)}) collective-permute-start(bf16[3,272,768]{2,1,0:T(8,128)(2,1)S(1)} %add_convert_fusion.1.dm_ref), channel_id=1, source_target_pairs={{0,1},{1,0},{2,3},{3,2},{4,5},{5,4},{6,7},{7,6},{8,9},{9,8},{10,11... | collective-permute-start | bytes 3760136 | tf_op jit(solution)/shard_map/ppermute | solution.py:759
  170.7 28.3 %collective-permute-start.41 = (bf16[4,3,48,768]{3,2,1,0:T(8,128)(2,1)}, bf16[4,3,48,768]{3,2,1,0:T(8,128)(2,1)S(1)}, u32[]{:S(2)}, u32[]{:S(2)}) collective-permute-start(bf16[4,3,48,768]{3,2,1,0:T(8,128)(2,1)} %get-tuple-element.164), channel_id=1, source_target_pairs={{0,4},{2,6},{4,0},{6,2},{8,12},{10,14},{12,8},{14,10},{16,20},{18,... | collective-permute-start | bytes 2654216 | tf_op jit(solution)/shard_map/ppermute | solution.py:731
  204.7 29.8 %collective-permute-start.44 = (bf16[3,272,768]{2,1,0:T(8,128)(2,1)S(1)}, bf16[3,272,768]{2,1,0:T(8,128)(2,1)}, u32[]{:S(2)}, u32[]{:S(2)}) collective-permute-start(bf16[3,272,768]{2,1,0:T(8,128)(2,1)S(1)} %add_convert_fusion.zm_ref), channel_id=1, source_target_pairs={{0,1},{1,0},{2,3},{3,2},{4,5},{5,4},{6,7},{7,6},{8,9},{9,8},{10,11... | collective-permute-start | bytes 3760136 | tf_op jit(solution)/shard_map/ppermute | solution.py:759
  205.3 26.7 %collective-permute-start.46 = (bf16[4,3,48,768]{3,2,1,0:T(8,128)(2,1)}, bf16[4,3,48,768]{3,2,1,0:T(8,128)(2,1)}, u32[]{:S(2)}, u32[]{:S(2)}) collective-permute-start(bf16[4,3,48,768]{3,2,1,0:T(8,128)(2,1)} %get-tuple-element.174), channel_id=1, source_target_pairs={{0,4},{2,6},{4,0},{6,2},{8,12},{10,14},{12,8},{14,10},{16,20},{18,... | collective-permute-start | bytes 2654216 | tf_op jit(solution)/shard_map/ppermute | solution.py:731
  207.0 25.0 %collective-permute-start.45 = (bf16[2,3,48,768]{3,2,1,0:T(8,128)(2,1)}, bf16[2,3,48,768]{3,2,1,0:T(8,128)(2,1)}, u32[]{:S(2)}, u32[]{:S(2)}) collective-permute-start(bf16[2,3,48,768]{3,2,1,0:T(8,128)(2,1)} %add_convert_fusion.6), channel_id=1, source_target_pairs={{0,8},{2,10},{4,12},{6,14},{8,0},{10,2},{12,4},{14,6},{16,24},{18,... | collective-permute-start | bytes 1327112 | tf_op jit(solution)/shard_map/ppermute | solution.py:731
  207.9 43.4 %collective-permute-start.50 = (bf16[4,3,48,768]{3,2,1,0:T(8,128)(2,1)}, bf16[4,3,48,768]{3,2,1,0:T(8,128)(2,1)}, u32[]{:S(2)}, u32[]{:S(2)}) collective-permute-start(bf16[4,3,48,768]{3,2,1,0:T(8,128)(2,1)} %get-tuple-element.187), channel_id=1, source_target_pairs={{0,4},{2,6},{4,0},{6,2},{8,12},{10,14},{12,8},{14,10},{16,20},{18,... | collective-permute-start | bytes 2654216 | tf_op jit(solution)/shard_map/ppermute | solution.py:731
  234.5 16.7 %collective-permute-start.47 = (f32[2,768]{1,0:T(2,128)S(1)}, f32[2,768]{1,0:T(2,128)S(1)}, u32[]{:S(2)}, u32[]{:S(2)}) collective-permute-start(f32[2,768]{1,0:T(2,128)S(1)} %slice.181), channel_id=1, source_target_pairs={{0,1},{1,0},{2,3},{3,2},{4,5},{5,4},{6,7},{7,6},{8,9},{9,8},{10,11... | collective-permute-start | bytes 18440 | tf_op jit(solution)/shard_map/ppermute | solution.py:759
  240.5 45.9 %collective-permute-start.51 = (bf16[3,272,768]{2,1,0:T(8,128)(2,1)S(1)}, bf16[3,272,768]{2,1,0:T(8,128)(2,1)}, u32[]{:S(2)}, u32[]{:S(2)}) collective-permute-start(bf16[3,272,768]{2,1,0:T(8,128)(2,1)S(1)} %copy-done.21), channel_id=1, source_target_pairs={{0,1},{1,0},{2,3},{3,2},{4,5},{5,4},{6,7},{7,6},{8,9},{9,8},{10,11... | collective-permute-start | bytes 3760136 | tf_op jit(solution)/shard_map/ppermute | solution.py:759
  251.3 19.0 %collective-permute-start.54 = (bf16[4,4,48,384]{3,2,1,0:T(8,128)(2,1)}, bf16[4,4,48,384]{3,2,1,0:T(8,128)(2,1)}, u32[]{:S(2)}, u32[]{:S(2)}) collective-permute-start(bf16[4,4,48,384]{3,2,1,0:T(8,128)(2,1)} %get-tuple-element.199), channel_id=1, source_target_pairs={{0,2},{2,0},{4,6},{6,4},{8,10},{10,8},{12,14},{14,12},{16,18},{18,... | collective-permute-start | bytes 1769480 | tf_op jit(solution)/shard_map/ppermute | solution.py:731
  266.9 25.3 %collective-permute-start.59 = (bf16[2,3,48,768]{3,2,1,0:T(8,128)(2,1)}, bf16[2,3,48,768]{3,2,1,0:T(8,128)(2,1)}, u32[]{:S(2)}, u32[]{:S(2)}) collective-permute-start(bf16[2,3,48,768]{3,2,1,0:T(8,128)(2,1)} %add_convert_fusion.4), channel_id=1, source_target_pairs={{0,8},{2,10},{4,12},{6,14},{8,0},{10,2},{12,4},{14,6},{16,24},{18,... | collective-permute-start | bytes 1327112 | tf_op jit(solution)/shard_map/ppermute | solution.py:731
  267.0 25.2 %collective-permute-start.57 = (bf16[3,48,768]{2,1,0:T(8,128)(2,1)}, bf16[3,48,768]{2,1,0:T(8,128)(2,1)}, u32[]{:S(2)}, u32[]{:S(2)}) collective-permute-start(bf16[3,48,768]{2,1,0:T(8,128)(2,1)} %fusion.3), channel_id=1, source_target_pairs={{0,16},{2,18},{4,20},{6,22},{8,24},{10,26},{12,28},{14,30},{16,0},... | collective-permute-start | bytes 663560 | tf_op jit(solution)/shard_map/ppermute | solution.py:731
  270.3 28.9 %collective-permute-start.56 = (bf16[4,4,48,384]{3,2,1,0:T(8,128)(2,1)}, bf16[4,4,48,384]{3,2,1,0:T(8,128)(2,1)}, u32[]{:S(2)}, u32[]{:S(2)}) collective-permute-start(bf16[4,4,48,384]{3,2,1,0:T(8,128)(2,1)} %add_convert_fusion.2), channel_id=1, source_target_pairs={{0,4},{2,6},{4,0},{6,2},{8,12},{10,14},{12,8},{14,10},{16,20},{18,... | collective-permute-start | bytes 1769480 | tf_op jit(solution)/shard_map/ppermute | solution.py:731
  295.2 22.4 %collective-permute-start.63 = (bf16[3,48,768]{2,1,0:T(8,128)(2,1)}, bf16[3,48,768]{2,1,0:T(8,128)(2,1)}, u32[]{:S(2)}, u32[]{:S(2)}) collective-permute-start(bf16[3,48,768]{2,1,0:T(8,128)(2,1)} %fusion.4), channel_id=1, source_target_pairs={{0,16},{2,18},{4,20},{6,22},{8,24},{10,26},{12,28},{14,30},{16,0},... | collective-permute-start | bytes 663560 | tf_op jit(solution)/shard_map/ppermute | solution.py:731
  299.1 17.4 %collective-permute-start.62 = (f32[3,48,768]{2,1,0:T(8,128)S(1)}, f32[3,48,768]{2,1,0:T(8,128)}, u32[]{:S(2)}, u32[]{:S(2)}) collective-permute-start(f32[3,48,768]{2,1,0:T(8,128)S(1)} %bitcast_add_fusion.2), channel_id=1, source_target_pairs={{0,2},{2,0},{4,6},{6,4},{8,10},{10,8},{12,14},{14,12},{16,18},{18,... | collective-permute-start | bytes 1327112 | tf_op jit(solution)/shard_map/ppermute | solution.py:731
  (110 other events, 1258.5 us)
where the time goes:
time: 329 us; the launch traced here: 327 us
  Pallas kernels  110 us (33%)
  waiting for transfers between devices  91 us (28%)
  starting transfers between devices  54.3 us (17%)
  local copies, waits for them, and re-layouts  35.7 us (11%)
  other arithmetic  33.8 us (10%)
    ppermute x60, waiting for transfers between devices, swap(): return lax.ppermute(value, axis, [(i, i ^ mask) for i in range(size)])  85.6 us
    ppermute x60, starting transfers between devices, swap(): return lax.ppermute(value, axis, [(i, i ^ mask) for i in range(size)])  48.1 us
    pallas_call x2, Pallas kernels, weight_grad(): pl.pallas_call(functools.partial(k_weight_grad, n_left=len(left), n_out=n...  26.5 us
    pallas_call x1, Pallas kernels, attend_back(): pl.pallas_call(functools.partial(k_attend_back, scale=scale), grid_spec=g...  20.4 us
    pallas_call x1, local copies, waits for them, and re-layouts, experts_back(): pl.pallas_call(functools.partial(k_back, n_left=len(left), n_up=len(ups),...  15 us
    pallas_call x1, Pallas kernels, experts_down(): pl.pallas_call(functools.partial(k_down, own=own), grid_spec=grid_spec, o...  10.8 us
    pallas_call x1, Pallas kernels, experts_up(): pl.pallas_call(functools.partial(k_up, n_left=len(b)), grid_spec=grid_spe...  10.2 us
    pallas_call x1, Pallas kernels, attn_grad(): pl.pallas_call(functools.partial(k_attn_grad, base=base), grid_spec=grid_...  9.11 us
  transfers between devices with their start and end apart: 66, of which 24 were waited for; matrix products, arithmetic and copies ran while one was open for 14% of the time, Pallas kernels for 34%

commit v1 on v0

--- a/solution.py
+++ b/solution.py
@@ -567,17 +567,21 @@
 
 
 def k_attend_back(
-    len_ref, dm_ref, dp_ref, h_ref, g_ref, tok_ref, q_ref, k_ref, v_ref, w_ref, wo_ref, vec_ref,
-    dh_ref, dy_ref, dqkv_ref, da_ref, sums_ref, bias_ref, *, scale,
+    len_ref, slot_ref, dm_ref, dp_ref, h_ref, g_ref, tok_ref, a_ref, c_ref, q_ref, k_ref, v_ref,
+    w_ref, wo_ref, vec_ref, dh_ref, da_ref, one_ref, two_ref, bias_ref, *rest, scale,
 ):
+    dqkv, acc, stage, sems = rest[-4:]
+    outs = rest[:-4]
     rows, width = dh_ref.shape[1:]
     cols = q_ref.shape[3]
     i = pl.program_id(0)
 
     @pl.when(i == 0)
     def _():
-        sums_ref[...] = jnp.zeros_like(sums_ref)
+        one_ref[...] = jnp.zeros_like(one_ref)
+        two_ref[...] = jnp.zeros_like(two_ref)
         bias_ref[...] = jnp.zeros_like(bias_ref)
+        acc[...] = jnp.zeros_like(acc)
 
     def add_rows(ref, at, value):
         ref[at : at + 1, :] += jnp.sum(value, axis=0, keepdims=True)
@@ -587,10 +591,9 @@
     dh = g_ref[0].astype(F32) + norm_back(db, hat, spread, vec_ref[3:4, :])
     dh_ref[0] = dh
     dy = dh.astype(BF)
-    dy_ref[0] = dy
-    add_rows(sums_ref, 0, db * hat)
-    add_rows(sums_ref, 1, db)
-    add_rows(sums_ref, 2, dy.astype(F32))
+    add_rows(two_ref, 0, db * hat)
+    add_rows(two_ref, 1, db)
+    add_rows(two_ref, 2, dy.astype(F32))
     dctx = dot(dy, wo_ref[0], NN).astype(BF)
     valid = lax.broadcasted_iota(jnp.int32, (rows, 1), 0) < IMG + len_ref[i]
     low = lax.broadcasted_iota(jnp.int32, (1, LANES), 1) < HDIM
@@ -608,37 +611,47 @@
             dp = dot(v * only, dc, NT)
             ds = (p * (dp - jnp.sum(p * dp, axis=0, keepdims=True))).astype(BF)
             parts.append((dot(ds, k, TN), dot(ds, q, NN), dot(p.astype(BF), dc, NN)))
-        dqkv_ref[0, 0, :, at] = (jnp.where(low, parts[0][0], parts[1][0]) * scale).astype(BF)
-        dqkv_ref[0, 1, :, at] = (jnp.where(low, parts[0][1], parts[1][1]) * scale).astype(BF)
-        dqkv_ref[0, 2, :, at] = jnp.where(low, parts[0][2], parts[1][2]).astype(BF)
-    da = dot(dqkv_ref[0, 0], w_ref[0], NT)
-    da += dot(dqkv_ref[0, 1], w_ref[1], NT)
-    da += dot(dqkv_ref[0, 2], w_ref[2], NT)
-    add_rows(bias_ref, 0, dqkv_ref[0, 0].astype(F32))
-    add_rows(bias_ref, 1, dqkv_ref[0, 2].astype(F32))
+        dqkv[0, :, at] = (jnp.where(low, parts[0][0], parts[1][0]) * scale).astype(BF)
+        dqkv[1, :, at] = (jnp.where(low, parts[0][1], parts[1][1]) * scale).astype(BF)
+        dqkv[2, :, at] = jnp.where(low, parts[0][2], parts[1][2]).astype(BF)
+    da = dot(dqkv[0], w_ref[0], NT)
+    da += dot(dqkv[1], w_ref[1], NT)
+    da += dot(dqkv[2], w_ref[2], NT)
+    add_rows(bias_ref, 0, dqkv[0].astype(F32))
+    add_rows(bias_ref, 1, dqkv[2].astype(F32))
     hat, _ = normed(tok_ref[0].astype(F32))
-    add_rows(sums_ref, 3, da * hat)
-    add_rows(sums_ref, 4, da)
+    add_rows(one_ref, 0, da * hat)
+    add_rows(one_ref, 1, da)
     da_ref[0] = da.astype(BF)
-
-
-def attend_back(text_len, mine, theirs, h, g, tokens, qkv, weights, w_out, vectors, scale):
+    for t in range(3):
+        acc[t] += dot(a_ref[0], dqkv[t], TN)
+    acc[3] += dot(dy, c_ref[0], TN)
+
+    @pl.when(i == pl.num_programs(0) - 1)
+    def _():
+        write_chunks(slot_ref, 0, acc, stage, outs, sems)
+
+
+def attend_back(
+    text_len, slots, mine, theirs, h, g, tokens, a, ctx, qkv, weights, w_out, vectors, chunk, n_out, scale
+):
     items, rows, width = h.shape
     cols = qkv.shape[3]
     block = per_item((1, rows, width))
     grid_spec = pltpu.PrefetchScalarGridSpec(
-        num_scalar_prefetch=1,
+        num_scalar_prefetch=2,
         grid=(items,),
-        in_specs=[block] * 5
+        in_specs=[block] * 6
+        + [per_item((1, rows, cols))]
         + qkv_specs(rows, cols)
         + [full(weights.shape), full(w_out.shape), full(vectors.shape)],
-        out_specs=[
-            block,
-            block,
-            per_item((1, 3, rows, cols)),
-            block,
-            full((5, width)),
-            full((2, cols)),
+        out_specs=[block, block, full((2, width)), full((3, width)), full((2, cols))]
+        + [ANY] * n_out,
+        scratch_shapes=[
+            pltpu.VMEM((3, rows, cols), BF),
+            pltpu.VMEM((4, width, cols), F32),
+            pltpu.VMEM((chunk[0] * n_out,) + chunk[1:], BF),
+            pltpu.SemaphoreType.DMA((n_out,)),
         ],
     )
     return pl.pallas_call(
@@ -647,62 +660,15 @@
         out_shape=[
             jax.ShapeDtypeStruct((items, rows, width), F32),
             jax.ShapeDtypeStruct((items, rows, width), BF),
-            jax.ShapeDtypeStruct((items, 3, rows, cols), BF),
-            jax.ShapeDtypeStruct((items, rows, width), BF),
-            jax.ShapeDtypeStruct((5, width), F32),
+            jax.ShapeDtypeStruct((2, width), F32),
+            jax.ShapeDtypeStruct((3, width), F32),
             jax.ShapeDtypeStruct((2, cols), F32),
-        ],
+        ]
+        + [jax.ShapeDtypeStruct(chunk, BF)] * n_out,
         compiler_params=params(),
         cost_estimate=SHORT,
         name="attend_back",
-    )(text_len, mine, theirs, h, g, tokens, qkv, qkv, qkv, weights, w_out, vectors)
-
-
-def k_attn_grad(slot_ref, a_ref, d_ref, y_ref, c_ref, *rest, base):
-    acc, stage, sems = rest[-3:]
-    outs = rest[:-3]
-    i = pl.program_id(0)
-
-    @pl.when(i == 0)
-    def _():
-        acc[...] = jnp.zeros_like(acc)
-
-    for t in range(4):
-        left, right = (a_ref[0], d_ref[0, t]) if t < 3 else (y_ref[0], c_ref[0])
-        acc[t] += dot(left, right, TN)
-
-    @pl.when(i == pl.num_programs(0) - 1)
-    def _():
-        write_chunks(slot_ref, base, acc, stage, outs, sems)
-
-
-def attn_grad(slots, base, a, dqkv, dy, ctx, chunk, n_out):
-    items, rows, width = a.shape
-    cols = ctx.shape[2]
-    grid_spec = pltpu.PrefetchScalarGridSpec(
-        num_scalar_prefetch=1,
-        grid=(items,),
-        in_specs=[
-            per_item((1, rows, width)),
-            per_item((1, 3, rows, cols)),
-            per_item((1, rows, width)),
-            per_item((1, rows, cols)),
-        ],
-        out_specs=[ANY] * n_out,
-        scratch_shapes=[
-            pltpu.VMEM((4, width, cols), F32),
-            pltpu.VMEM((chunk[0] * n_out,) + chunk[1:], BF),
-            pltpu.SemaphoreType.DMA((n_out,)),
-        ],
-    )
-    return pl.pallas_call(
-        functools.partial(k_attn_grad, base=base),
-        grid_spec=grid_spec,
-        out_shape=[jax.ShapeDtypeStruct(chunk, BF)] * n_out,
-        compiler_params=params(),
-        cost_estimate=SHORT,
-        name="attn_grad",
-    )(slots, a, dqkv, dy, ctx)
+    )(text_len, slots, mine, theirs, h, g, tokens, a, ctx, qkv, qkv, qkv, weights, w_out, vectors)
 
 
 def k_token_grad(dh_ref, dm_ref, dp_ref, tok_ref, vec_ref, o_ref):
@@ -753,7 +719,7 @@
     me = lax.axis_index("dp")
     core = me % 2
     by_permute = dp == 16 and share % SUB == 0
-    masks = [m for m in (1, 2, 4, 8, 16, 32, 64, 128) if m < dp]
+    masks = [m for m in (1, 128, 64, 32, 16, 8, 4, 2) if m < dp]
 
     def peer(value):
         return lax.ppermute(value, "rep", [(i, i ^ 1) for i in range(rep)])
@@ -876,21 +842,22 @@
         def middle(parts, core_slot, got, *others):
             keep, got = tie(parts[2 * core_slot], got, *others), tie(got, *others)
             both = keep[2:4].astype(F32) + got[2:4].astype(F32)
-            return keep, got, dp_swap(both.astype(BF), 4)
-
-        def last(state, *others):
-            keep, got, mid = state
+            return keep, got, both.astype(BF)
+
+        def last(state, mid, *others):
+            keep, got, _ = state
             mid = tie(mid, *others)
             part = keep[1].astype(F32) + got[1].astype(F32) + mid[1].astype(F32)
-            return keep, got, mid, dp_swap(part.astype(BF), 8)
-
-        def total(state):
-            keep, got, mid, end = state
+            return keep, got, mid, part.astype(BF)
+
+        def total(state, end, *others, planes=slice(None)):
+            keep, got, mid, _ = state
+            end = tie(end, *others)
             return (
-                keep[0].astype(F32)
-                + got[0].astype(F32)
-                + mid[0].astype(F32)
-                + end.astype(F32)
+                keep[0, planes].astype(F32)
+                + got[0, planes].astype(F32)
+                + mid[0, planes].astype(F32)
+                + end[planes].astype(F32)
             )
 
         stage = stage + [x3d]
@@ -898,11 +865,14 @@
     db_own, db_other, du, grad_b_up = experts_back(
         tie(experts_two, *stage), ffn_off, cots, slope, up_pieces, down_pieces, items
     )
-    db = add_low(db_own, partner(db_other))
-    stage = [db]
-    if by_permute:
-        stage = stage + [dn1]
-        dm1 = middle(down_grad, 1, dn1, *stage)
+    stage = [du]
+    if by_permute:
+        d1 = middle(down_grad, 1, dn1, du)
+        stage = [d1[2]]
+    db = add_low(db_own, partner(tie(db_other, *stage)))
+    stage = stage + [db]
+    if by_permute:
+        df1 = dp_swap(tie(d1[2], *stage), 4)
         dn0 = near(down_grad, 0, *stage)
     db_theirs = peer(tie(db, *stage))
     *up_grad, _ = weight_grad(
@@ -910,45 +880,50 @@
     )
     stage = [up_grad[0]]
     if by_permute:
-        stage = stage + [dm1[2]]
+        stage = stage + [df1]
         un1 = near(up_grad, 1, *stage)
-        de1 = last(dm1, *stage)
+        d1 = last(d1, df1, *stage)
+        dg1 = dp_swap(d1[3], 8)
     z_own, z_other = experts_down(
         tie(experts_two, *stage), ffn_off, act, down_pieces, rows, items
     )
     stage = [z_own, db_theirs]
     if by_permute:
-        stage = stage + [dn0, de1[3]]
-        dm0 = middle(down_grad, 0, dn0, *stage)
+        d0 = middle(down_grad, 0, dn0, *stage)
+        stage = stage + [d0[2], dg1]
+    z = add_low(z_own, partner(tie(z_other, *stage)))
+    stage = stage + [z]
+    z_theirs = peer(tie(z, *stage))
+    if by_permute:
+        df0 = dp_swap(tie(d0[2], *stage), 4)
         un0 = near(up_grad, 0, *stage)
-    z = add_low(z_own, partner(tie(z_other, *stage)))
-    z_theirs = peer(z)
-
-    dh, dy, dqkv, da, sums, bias_sums = attend_back(
-        tie(text_len, z), db, db_theirs, h, cots[0], tok, qkv, attn_w, out_w, vectors, scale
+
+    dh, da, norm_one, norm_two, bias_sums, *attn_parts = attend_back(
+        tie(text_len, *stage), slots, db, db_theirs, h, cots[0], tok, a, ctx, qkv, attn_w, out_w, vectors,
+        attn_chunk, n_out, scale,
     )
     stage = [bias_sums, z_theirs]
     if by_permute:
-        stage = stage + [dm0[2], un1]
-        um1 = middle(up_grad, 1, un1, *stage)
-        de0 = last(dm0, *stage)
-    da_theirs = peer(tie(da, *stage))
-    first_norm = tie(sums[3:5], *stage)
-    first_norm_theirs = peer(first_norm)
-    attn_parts = attn_grad(tie(slots, *stage), 0, a, dqkv, dy, ctx, attn_chunk, n_out)
-
-    stage = [attn_parts[0], first_norm_theirs]
+        u1 = middle(up_grad, 1, un1, *stage)
+        stage = stage + [u1[2], df0]
+        uf1 = dp_swap(tie(u1[2], *stage), 4)
+        d0 = last(d0, df0, *stage)
+        dg0 = dp_swap(d0[3], 8)
+    da_theirs = peer(tie(da, bias_sums, z_theirs))
+    norm_one_theirs = peer(tie(norm_one, *stage))
+    attn_parts = [tie(v, *stage) for v in attn_parts]
+
     up_pair = jnp.zeros((2, e_count, hidden), F32)
     up_pair = lax.dynamic_update_slice_in_dim(up_pair, grad_b_up[None], core, 0)
     small = jnp.concatenate(
         [
-            (first_norm + first_norm_theirs).reshape(-1),
-            sums[0:3].reshape(-1),
-            grad_b_down.reshape(-1),
-            up_pair.reshape(-1),
-            bias_sums.reshape(-1),
+            norm_one + norm_one_theirs,
+            norm_two,
+            grad_b_down,
+            up_pair.reshape(-1, width),
+            bias_sums.reshape(-1, width),
         ]
-    ).reshape(-1, LANES)
+    )
     steps = list(masks)
 
     def add_step(*others):
@@ -958,30 +933,46 @@
         small = small + got
         return got
 
-    if by_permute:
-        send = add_low(attn_parts[1], partner(attn_parts[3]))
-        keep = add_low(attn_parts[0], partner(attn_parts[2]))
-        stage = stage + [um1[2], de0[3], un0]
+    stage = [norm_one_theirs]
+    if by_permute:
+        u0 = middle(up_grad, 0, un0, *stage)
+        stage = stage + [u0[2]]
+        send = add_low(tie(attn_parts[1], *stage), partner(attn_parts[3]))
+        keep = add_low(tie(attn_parts[0], *stage), partner(attn_parts[2]))
         an = near([keep, send], 0, *stage)
-        ue1 = last(um1, *stage)
-        um0 = middle(up_grad, 0, un0, *stage)
-        down_other = total(tie(de1, *stage))
-        down_got = partner(down_other)
+        uf0 = dp_swap(tie(u0[2], *stage), 4)
+        stage = stage + [keep, send]
     got = add_step(*stage)
     output = finish_output(tie(experts, *stage), h, z, z_theirs, b_down, seq)
     stage = [output, got]
     if by_permute:
-        stage = stage + [down_got]
-        down_mine = total(tie(de0, *stage))
+        stage = stage + [uf1, dg0]
+        u1 = last(u1, uf1, *stage)
+        ug1 = dp_swap(u1[3], 8)
+        stage = [u1[3], got]
+        got = add_step(*stage)
+        down_other = total(d1, dg1, *stage)
+        down_got = partner(down_other)
+        u0 = last(u0, uf0, *stage)
+        ug0 = dp_swap(u0[3], 8)
+        stage = [u0[3], down_other, da_theirs]
+        a0 = middle([keep, send], 0, an, *stage)
+        stage = stage + [a0[2]]
+        af = dp_swap(tie(a0[2], *stage), 4)
+        down_mine = total(d0, dg0, *stage)
+        stage = stage + [down_mine]
+    else:
+        got = add_step(*stage)
+    stage = [got, *stage]
+    grad_tokens = token_grad(dh, da, da_theirs, tok, tie(vectors, *stage), seq)
+    stage = [grad_tokens]
     got = add_step(*stage)
-    grad_tokens = token_grad(dh, da, da_theirs, tok, tie(vectors, *stage), seq)
-    stage = [grad_tokens, got]
-    if by_permute:
-        stage = stage + [um0[2], ue1[3]]
-        ue0 = last(um0, *stage)
-        up_other = total(tie(ue1, *stage))
+    if by_permute:
+        up_other = total(u1, ug1, *stage)
         up_got = partner(up_other)
-    got = add_step(*stage)
+        a0 = last(a0, af, up_other, *stage)
+        stage = stage + [a0[3], got]
+        got = add_step(*stage)
 
     if by_permute:
 
@@ -990,12 +981,12 @@
             whole = lax.dynamic_update_slice_in_dim(whole, got, (1 - core) * hidden, 2)
             return lax.dynamic_update_slice_in_dim(whole, own, core * hidden, 2)
 
-        am = middle([keep, send], 0, an, up_other)
-        grad_w_down = joined(tie(down_mine, am[0]), down_got)
-        ae = last(am, grad_w_down)
-        grad_w_up = joined(total(ue0), up_got)
-        grad_attn = total(tie(ae, grad_w_up))
-        grad_w_qkv, grad_w_out = grad_attn[:3], grad_attn[3]
+        ag = dp_swap(a0[3], 8)
+        grad_w_down = joined(tie(down_mine, a0[3]), down_got)
+        grad_w_up = joined(total(u0, ug0, a0[3]), up_got)
+        ag = tie(ag, grad_w_up)
+        grad_w_qkv = total(a0, ag, planes=slice(0, 3))
+        grad_w_out = total(a0, ag, planes=3)
     else:
 
         def finish(chunk):
@@ -1009,20 +1000,12 @@
 
     while steps:
         add_step()
-    small = small.reshape(-1)
-    at = 0
-
-    def take(*shape):
-        nonlocal at
-        n = math.prod(shape)
-        piece = small[at : at + n].reshape(shape)
-        at += n
-        return piece
-
-    norm_one, norm_two, grad_b_out = take(2, width), take(2, width), take(width)
-    total_down = take(e_count, width)
-    total_up = jnp.moveaxis(take(2, e_count, hidden), 0, 1).reshape(e_count, 2 * hidden)
-    total_qv = take(2, cols)
+    at = 5 + e_count
+    end = at + e_count * hidden // width
+    total_up = jnp.concatenate(
+        [small[n : n + end - at].reshape(e_count, hidden) for n in (at, end)], axis=1
+    )
+    total_qv = small[2 * end - at :].reshape(2, cols)
     return (
         output,
         grad_tokens,
@@ -1031,10 +1014,10 @@
         grad_w_up,
         grad_w_down,
         total_qv,
-        grad_b_out,
+        small[4],
         total_up,
-        total_down,
-        jnp.concatenate([norm_one, norm_two], axis=0),
+        small[5:at],
+        small[:4],
     )
 
 

time: 329 us -> 301 us (0.915)
  waiting for transfers between devices: 91 us -> 68.1 us
  local copies, waits for them, and re-layouts: 35.7 us -> 18.9 us
  Pallas kernels: 110 us -> 123 us
    ppermute x60, waiting for transfers between devices: 85.6 us -> 65.3 us  [swap(): return lax.ppermute(value, axis, [(i, i ^ mask) for i in range(size)])]
    pallas_call x1 -> x0, local copies, waits for them, and re-layouts: 15 us -> none  [experts_back(): pl.pallas_call(functools.partial(k_back, n_left=len(left), n_up=len(ups),...]
    pallas_call x1, Pallas kernels: 9.11 us -> 15.9 us  [experts_back(): pl.pallas_call(functools.partial(k_back, n_left=len(left), n_up=len(ups),...]
    pallas_call x1, Pallas kernels: 20.4 us -> 26.8 us  [attend_back(): pl.pallas_call(functools.partial(k_attend_back, scale=scale), grid_spec=g...]
    unnamed x140 -> x147, local copies, waits for them, and re-layouts: 3.88 us -> 6.76 us
    add x5 -> x6, other arithmetic: 5.92 us -> 8.1 us  [the longest x5 8.1 us: total(): keep[0, planes].astype(F32) + got[0, planes].astype(F32)]
  transfers between devices with their start and end apart: 66 -> 66, of which waited for: 24 -> 23; matrix products, arithmetic and copies ran while one was open for 14% -> 14% of each run, Pallas kernels for 34% -> 41%
where the time goes in v1:
time: 301 us; the launch traced here: 300 us
  Pallas kernels  123 us (41%)
  waiting for transfers between devices  68.1 us (23%)
  starting transfers between devices  53.7 us (18%)
  other arithmetic  34 us (11%)
  local copies, waits for them, and re-layouts  18.9 us (6%)
    ppermute x60, waiting for transfers between devices, swap(): return lax.ppermute(value, axis, [(i, i ^ mask) for i in range(size)])  65.3 us
    ppermute x60, starting transfers between devices, swap(): return lax.ppermute(value, axis, [(i, i ^ mask) for i in range(size)])  48.2 us
    pallas_call x1, Pallas kernels, attend_back(): pl.pallas_call(functools.partial(k_attend_back, scale=scale), grid_spec=g...  26.8 us
    pallas_call x2, Pallas kernels, weight_grad(): pl.pallas_call(functools.partial(k_weight_grad, n_left=len(left), n_out=n...  26.4 us
    pallas_call x1, Pallas kernels, experts_back(): pl.pallas_call(functools.partial(k_back, n_left=len(left), n_up=len(ups),...  15.9 us
    pallas_call x1, Pallas kernels, experts_down(): pl.pallas_call(functools.partial(k_down, own=own), grid_spec=grid_spec, o...  10.8 us
    pallas_call x1, Pallas kernels, experts_up(): pl.pallas_call(functools.partial(k_up, n_left=len(b)), grid_spec=grid_spe...  10.2 us
    pallas_call x1, Pallas kernels, project(): pl.pallas_call(k_proj, grid_spec=grid_spec, out_shape=[jax.ShapeDtypeStru...  8.75 us
  transfers between devices with their start and end apart: 66, of which 23 were waited for; matrix products, arithmetic and copies ran while one was open for 14% of the time, Pallas kernels for 41%

profile of v1, /device:TPU:0, one launch (start us, length us, event | category | flops | bytes accessed | tf_op | source)
XLA Modules:
  0.0 299.6 jit_solution(17923149256072166798)
XLA Ops:
  2.2 3.8 %collective-permute-start.2 = (bf16[1,4,48,384]{3,2,1,0:T(8,128)(2,1)S(1)}, bf16[1,4,48,384]{3,2,1,0:T(8,128)(2,1)S(1)}, u32[]{:S(2)}, u32[]{:S(2)}) collective-permute-start(bf16[1,4,48,384]{3,2,1,0:T(8,128)(2,1)S(1)} %maximum_bitcast_fusion.rest_0_), channel_id=1, source_target_pairs={{0,16},{2,18},{4,20},{6,22},{8,24},{10,26},{12,28},{14,30},{16,0},... | collective-permute-start | bytes 442376 | tf_op jit(solution)/shard_map/ppermute | solution.py:697
  10.3 3.4 %collective-permute-done.2.rest_2_ = bf16[1,4,48,384]{3,2,1,0:T(8,128)(2,1)S(1)} collective-permute-done((bf16[1,4,48,384]{3,2,1,0:T(8,128)(2,1)S(1)}, bf16[1,4,48,384]{3,2,1,0:T(8,128)(2,1)S(1)}, u32[]{:S(2)}, u32[]{:S(2)}) %collective-permute-start.2) | collective-permute-done | bytes 147488 | tf_op jit(solution)/shard_map/ppermute | solution.py:697
  36.2 8.8 %project.1 = (bf16[3,272,768]{2,1,0:T(8,128)(2,1)}, bf16[3,3,272,384]{3,2,1,0:T(8,128)(2,1)}, bf16[3,768,384]{2,1,0:T(8,128)(2,1)}, bf16[1,768,384]{2,1,0:T(8,128)(2,1)}) custom-call(s32[16]{0:T(128)} %xor_multiply_fusion.1.off_ref, bf16[3,272,768]{2,1,0:T(8,128)(2,1)} %pad.10.tok_ref, f32[5,768]{1,0:T(8,128)} %stack.48.vec_ref, ...), custom_call_target="tpu_custom_call" | custom-call | flops 1 | bytes 1 | tf_op jit(solution)/shard_map/project/pallas_call | solution.py:138
  44.9 5.7 %collective-permute-done.17.rest_3_ = bf16[2,3,48,768]{3,2,1,0:T(8,128)(2,1)S(1)} collective-permute-done((bf16[2,3,48,768]{3,2,1,0:T(8,128)(2,1)S(1)}, bf16[2,3,48,768]{3,2,1,0:T(8,128)(2,1)S(1)}, u32[]{:S(2)}, u32[]{:S(2)}) %collective-permute-start.17) | collective-permute-done | bytes 442400 | tf_op jit(solution)/shard_map/ppermute | solution.py:697
  59.1 8.3 %attend.1.cm_ref.c_ref = bf16[3,272,384]{2,1,0:T(8,128)(2,1)} custom-call(s32[3]{0:T(128)} %len_ref.1, bf16[3,3,272,384]{3,2,1,0:T(8,128)(2,1)} %get-tuple-element.126.q_ref.k_ref.v_ref, bf16[3,3,272,384]{3,2,1,0:T(8,128)(2,1)} %get-tuple-element.126.q_ref.k_ref.v_ref, bf16[3,3,272,384]{3,2,1,0:T(8,128)(2,1)} %get-tuple-element.126.q_ref.k_ref.v_ref), custom_call_target="tpu_custom_call" | custom-call | flops 1 | bytes 1 | tf_op jit(solution)/shard_map/attend/pallas_call | solution.py:183
  77.8 3.8 %collective-permute-done.28.rest_8_ = bf16[2,3,48,768]{3,2,1,0:T(8,128)(2,1)S(1)} collective-permute-done((bf16[2,3,48,768]{3,2,1,0:T(8,128)(2,1)S(1)}, bf16[2,3,48,768]{3,2,1,0:T(8,128)(2,1)S(1)}, u32[]{:S(2)}, u32[]{:S(2)}) %collective-permute-start.28) | collective-permute-done | bytes 442400 | tf_op jit(solution)/shard_map/ppermute | solution.py:697
  85.2 5.5 %residual.1 = (f32[3,272,768]{2,1,0:T(8,128)}, bf16[3,272,768]{2,1,0:T(8,128)(2,1)}) custom-call(bf16[3,272,768]{2,1,0:T(8,128)(2,1)} %pad.10.tok_ref, bf16[3,272,384]{2,1,0:T(8,128)(2,1)} %attend.1.cm_ref.c_ref, bf16[3,272,384]{2,1,0:T(8,128)(2,1)} %copy-done.33, bf16[1,768,384]{2,1,0:T(8,128)(2,1)} %get-tuple-element.120.wm_ref.wo_ref, ...), custom_call_target="tpu_custom_call" | custom-call | flops 1 | bytes 1 | tf_op jit(solution)/shard_map/residual/pallas_call | solution.py:204
  98.3 10.2 %experts_up.1 = (bf16[6,288,768]{2,1,0:T(8,128)(2,1)}, bf16[6,288,768]{2,1,0:T(8,128)(2,1)}) custom-call(s32[2,6]{1,0:T(2,128)} %pad_add_fusion.1.e_ref, s32[16]{0:T(128)} %xor_multiply_fusion.off_ref, f32[3,768]{1,0:T(4,128)} %constant_dynamic-slice_fusion.bias_ref, bf16[3,272,768]{2,1,0:T(8,128)(2,1)} %get-tuple-element.141.rest_0_, ...), custom_call_target="tpu_custom_call" | custom-call | flops 1 | bytes 1 | tf_op jit(solution)/shard_map/experts_up/pallas_call | solution.py:328
  108.5 6.9 %collective-permute-done.33.rest_15_.rest_5_ = bf16[2,3,48,768]{3,2,1,0:T(8,128)(2,1)S(1)} collective-permute-done((bf16[2,3,48,768]{3,2,1,0:T(8,128)(2,1)}, bf16[2,3,48,768]{3,2,1,0:T(8,128)(2,1)S(1)}, u32[]{:S(2)}, u32[]{:S(2)}) %collective-permute-start.33) | collective-permute-done | bytes 442400 | tf_op jit(solution)/shard_map/ppermute | solution.py:697
  116.5 13.2 %weight_grad.2 = (bf16[4,3,48,768]{3,2,1,0:T(8,128)(2,1)}, bf16[4,3,48,768]{3,2,1,0:T(8,128)(2,1)}, bf16[4,3,48,768]{3,2,1,0:T(8,128)(2,1)}, bf16[4,3,48,768]{3,2,1,0:T(8,128)(2,1)}, f32[3,768]{1,0:T(4,128)}) custom-call(s32[2,6]{1,0:T(2,128)} %pad_add_fusion.1.e_ref, s32[16]{0:T(128)} %fusion.6.slot_ref, ...), custom_call_target="tpu_custom_call" | custom-call | flops 1 | bytes 1 | tf_op jit(solution)/shard_map/weight_grad/pallas_call | solution.py:387
  131.3 15.9 %experts_back.1 = (bf16[3,272,768]{2,1,0:T(8,128)(2,1)}, bf16[3,272,768]{2,1,0:T(8,128)(2,1)}, bf16[6,288,768]{2,1,0:T(8,128)(2,1)}, f32[3,768]{1,0:T(4,128)}) custom-call(s32[2,6]{1,0:T(2,128)} %pad_add_fusion.1.e_ref, s32[16]{0:T(128)} %xor_multiply_fusion.off_ref, bf16[6,288,768]{2,1,0:T(8,128)(2,1)} %get-tuple-element.152.slope_ref, ...), custom_call_target="tpu_custom_call" | custom-call | flops 1 | bytes 1 | tf_op jit(solution)/shard_map/experts_back/pallas_call | solution.py:474
  147.2 3.5 %collective-permute-done.37 = bf16[4,3,48,768]{3,2,1,0:T(8,128)(2,1)S(1)} collective-permute-done((bf16[4,3,48,768]{3,2,1,0:T(8,128)(2,1)}, bf16[4,3,48,768]{3,2,1,0:T(8,128)(2,1)S(1)}, u32[]{:S(2)}, u32[]{:S(2)}) %collective-permute-start.37) | collective-permute-done | bytes 884768 | tf_op jit(solution)/shard_map/ppermute | solution.py:697
  151.7 3.2 %collective-permute-done.38 = bf16[3,272,768]{2,1,0:T(8,128)(2,1)S(1)} collective-permute-done((bf16[3,272,768]{2,1,0:T(8,128)(2,1)}, bf16[3,272,768]{2,1,0:T(8,128)(2,1)S(1)}, u32[]{:S(2)}, u32[]{:S(2)}) %collective-permute-start.38) | collective-permute-done | bytes 1253408 | tf_op jit(solution)/shard_map/ppermute | solution.py:697
  159.9 13.2 %weight_grad.3 = (bf16[4,3,48,768]{3,2,1,0:T(8,128)(2,1)}, bf16[4,3,48,768]{3,2,1,0:T(8,128)(2,1)}, bf16[4,3,48,768]{3,2,1,0:T(8,128)(2,1)}, bf16[4,3,48,768]{3,2,1,0:T(8,128)(2,1)}, f32[3,768]{1,0:T(4,128)}) custom-call(s32[2,6]{1,0:T(2,128)} %pad_add_fusion.1.e_ref, s32[16]{0:T(128)} %fusion.6.slot_ref, bf16[6,288,768]{2,1,0:T(8,128)(2,1)} %get-tuple-element.153.right_ref, ...), custom_call_target="tpu_custom_call" | custom-call | flops 1 | bytes 1 | tf_op jit(solution)/shard_map/weight_grad/pallas_call | solution.py:387
  174.7 10.8 %experts_down.1 = (bf16[3,272,768]{2,1,0:T(8,128)(2,1)}, bf16[3,272,768]{2,1,0:T(8,128)(2,1)}) custom-call(s32[2,6]{1,0:T(2,128)} %pad_add_fusion.1.e_ref, s32[16]{0:T(128)} %xor_multiply_fusion.off_ref, bf16[6,288,768]{2,1,0:T(8,128)(2,1)} %get-tuple-element.142.right_ref.act_ref, bf16[2,3,48,768]{3,2,1,0:T(8,128)(2,1)} %copy-done.6, ...), custom_call_target="tpu_custom_call" | custom-call | flops 1 | bytes 1 | tf_op jit(solution)/shard_map/experts_down/pallas_call | solution.py:529
  187.9 3.2 %collective-permute-done.43 = bf16[3,272,768]{2,1,0:T(8,128)(2,1)S(1)} collective-permute-done((bf16[3,272,768]{2,1,0:T(8,128)(2,1)}, bf16[3,272,768]{2,1,0:T(8,128)(2,1)S(1)}, u32[]{:S(2)}, u32[]{:S(2)}) %collective-permute-start.43) | collective-permute-done | bytes 1253408 | tf_op jit(solution)/shard_map/ppermute | solution.py:697
  196.1 26.8 %attend_back.1 = (f32[3,272,768]{2,1,0:T(8,128)}, bf16[3,272,768]{2,1,0:T(8,128)(2,1)}, f32[2,768]{1,0:T(2,128)}, f32[3,768]{1,0:T(4,128)}, f32[2,384]{1,0:T(2,1...) custom-call(s32[3]{0:T(128)} %len_ref.1, ...), custom_call_target="tpu_custom_call" | custom-call | flops 1 | bytes 1 | tf_op jit(solution)/shard_map/attend_back/pallas_call | solution.py:657
  241.6 4.9 %finish_output.1 = bf16[3,261,768]{2,1,0:T(8,128)(2,1)} custom-call(s32[2,3]{1,0:T(2,128)} %copy-done.68, f32[3,272,768]{2,1,0:T(8,128)} %get-tuple-element.136.h_ref, bf16[3,272,768]{2,1,0:T(8,128)(2,1)} %copy-done.2, bf16[3,272,768]{2,1,0:T(8,128)(2,1)} %collective-permute-done.44.zp_ref, f32[3,768]{1,0:T(4,128)} %bias_ref.1), custom_call_target="tpu_custom_call" | custom-call | flops 1 | bytes 1 | tf_op jit(solution)/shard_map/finish_output/pallas_call | solution.py:559
  247.5 3.0 %collective-permute-done.53 = bf16[2,3,48,768]{3,2,1,0:T(8,128)(2,1)} collective-permute-done((bf16[2,3,48,768]{3,2,1,0:T(8,128)(2,1)}, bf16[2,3,48,768]{3,2,1,0:T(8,128)(2,1)}, u32[]{:S(2)}, u32[]{:S(2)}) %collective-permute-start.53) | collective-permute-done | bytes 442400 | tf_op jit(solution)/shard_map/ppermute | solution.py:697
  254.6 3.3 %collective-permute-done.56 = bf16[2,3,48,768]{3,2,1,0:T(8,128)(2,1)S(1)} collective-permute-done((bf16[2,3,48,768]{3,2,1,0:T(8,128)(2,1)}, bf16[2,3,48,768]{3,2,1,0:T(8,128)(2,1)S(1)}, u32[]{:S(2)}, u32[]{:S(2)}) %collective-permute-start.56) | collective-permute-done | bytes 442400 | tf_op jit(solution)/shard_map/ppermute | solution.py:697
  260.4 9.2 %collective-permute-done.55 = f32[15,768]{1,0:T(8,128)S(1)} collective-permute-done((f32[15,768]{1,0:T(8,128)S(1)}, f32[15,768]{1,0:T(8,128)S(1)}, u32[]{:S(2)}, u32[]{:S(2)}) %collective-permute-start.55) | collective-permute-done | bytes 46112 | tf_op jit(solution)/shard_map/ppermute | solution.py:697
  274.2 5.7 %token_grad.1 = f32[3,261,768]{2,1,0:T(8,128)} custom-call(f32[3,272,768]{2,1,0:T(8,128)} %get-tuple-element.201.dh_ref, bf16[3,272,768]{2,1,0:T(8,128)(2,1)} %get-tuple-element.203.dm_ref, bf16[3,272,768]{2,1,0:T(8,128)(2,1)} %collective-permute-done.51.dp_ref, bf16[3,272,768]{2,1,0:T(8,128)(2,1)} %pad.10.tok_ref, f32[5,768]{1,0:T(8,128)} %stack.48.vec_ref), custom_call_target="tpu_custom_call" | custom-call | flops 1 | bytes 1 | tf_op jit(solution)/shard_map/token_grad/pallas_call | solution.py:684
  282.4 3.2 %collective-permute-done.64 = f32[15,768]{1,0:T(8,128)S(1)} collective-permute-done((f32[15,768]{1,0:T(8,128)S(1)}, f32[15,768]{1,0:T(8,128)S(1)}, u32[]{:S(2)}, u32[]{:S(2)}) %collective-permute-start.64) | collective-permute-done | bytes 46112 | tf_op jit(solution)/shard_map/ppermute | solution.py:697
  288.1 2.9 collective-permute-done.65
  (331 shorter events, 119.8 us)
Async XLA Ops:
  0.7 33.4 %collective-permute-start = (bf16[3,261,768]{2,1,0:T(8,128)(2,1)}, bf16[3,261,768]{2,1,0:T(8,128)(2,1)}, u32[]{:S(2)}, u32[]{:S(2)}) collective-permute-start(bf16[3,261,768]{2,1,0:T(8,128)(2,1)} %param.33), channel_id=1, source_target_pairs={{0,2},{2,0},{4,6},{6,4},{8,10},{10,8},{12,14},{14,12},{16,18},{18,... | collective-permute-start | bytes 3608072 | tf_op jit(solution)/shard_map/ppermute | solution.py:697
  28.5 22.1 %collective-permute-start.17 = (bf16[2,3,48,768]{3,2,1,0:T(8,128)(2,1)S(1)}, bf16[2,3,48,768]{3,2,1,0:T(8,128)(2,1)S(1)}, u32[]{:S(2)}, u32[]{:S(2)}) collective-permute-start(bf16[2,3,48,768]{3,2,1,0:T(8,128)(2,1)S(1)} %pad_maximum_fusion.rest_2_), channel_id=1, source_target_pairs={{0,8},{2,10},{4,12},{6,14},{8,0},{10,2},{12,4},{14,6},{16,24},{18,... | collective-permute-start | bytes 1327112 | tf_op jit(solution)/shard_map/ppermute | solution.py:697
  29.4 21.2 %collective-permute-start.18 = (bf16[2,3,48,768]{3,2,1,0:T(8,128)(2,1)S(1)}, bf16[2,3,48,768]{3,2,1,0:T(8,128)(2,1)S(1)}, u32[]{:S(2)}, u32[]{:S(2)}) collective-permute-start(bf16[2,3,48,768]{3,2,1,0:T(8,128)(2,1)S(1)} %pad_maximum_fusion.rest_2_), channel_id=1, source_target_pairs={{0,16},{2,18},{4,20},{6,22},{8,24},{10,26},{12,28},{14,30},{16,0},... | collective-permute-start | bytes 1327112 | tf_op jit(solution)/shard_map/ppermute | solution.py:697
  31.4 19.2 %collective-permute-start.19 = (bf16[2,3,48,768]{3,2,1,0:T(8,128)(2,1)S(1)}, bf16[2,3,48,768]{3,2,1,0:T(8,128)(2,1)S(1)}, u32[]{:S(2)}, u32[]{:S(2)}) collective-permute-start(bf16[2,3,48,768]{3,2,1,0:T(8,128)(2,1)S(1)} %pad_maximum_fusion.rest_2_), channel_id=1, source_target_pairs={{0,4},{2,6},{4,0},{6,2},{8,12},{10,14},{12,8},{14,10},{16,20},{18,... | collective-permute-start | bytes 1327112 | tf_op jit(solution)/shard_map/ppermute | solution.py:697
  32.3 20.8 %collective-permute-start.21 = (bf16[2,3,48,768]{3,2,1,0:T(8,128)(2,1)S(1)}, bf16[2,3,48,768]{3,2,1,0:T(8,128)(2,1)S(1)}, u32[]{:S(2)}, u32[]{:S(2)}) collective-permute-start(bf16[2,3,48,768]{3,2,1,0:T(8,128)(2,1)S(1)} %pad_maximum_fusion.1.rest_10_.rest_0_), channel_id=1, source_target_pairs={{0,4},{2,6},{4,0},{6,2},{8,12},{10,14},{12,8},{14,10},{16,20},{18,... | collective-permute-start | bytes 1327112 | tf_op jit(solution)/shard_map/ppermute | solution.py:697
  68.0 16.3 %collective-permute-start.26 = (bf16[3,272,384]{2,1,0:T(8,128)(2,1)}, bf16[3,272,384]{2,1,0:T(8,128)(2,1)S(1)}, u32[]{:S(2)}, u32[]{:S(2)}) collective-permute-start(bf16[3,272,384]{2,1,0:T(8,128)(2,1)} %attend.1.cm_ref.c_ref), channel_id=1, source_target_pairs={{0,1},{1,0},{2,3},{3,2},{4,5},{5,4},{6,7},{7,6},{8,9},{9,8},{10,11... | collective-permute-start | bytes 1880072 | tf_op jit(solution)/shard_map/ppermute | solution.py:725
  70.0 22.1 %collective-permute-start.30 = (bf16[2,3,48,768]{3,2,1,0:T(8,128)(2,1)S(1)}, bf16[2,3,48,768]{3,2,1,0:T(8,128)(2,1)}, u32[]{:S(2)}, u32[]{:S(2)}) collective-permute-start(bf16[2,3,48,768]{3,2,1,0:T(8,128)(2,1)S(1)} %pad_maximum_fusion.1.rest_10_.rest_0_), channel_id=1, source_target_pairs={{0,16},{2,18},{4,20},{6,22},{8,24},{10,26},{12,28},{14,30},{16,0},... | collective-permute-start | bytes 1327112 | tf_op jit(solution)/shard_map/ppermute | solution.py:697
  71.4 20.9 %collective-permute-start.31 = (bf16[2,3,48,768]{3,2,1,0:T(8,128)(2,1)S(1)}, bf16[2,3,48,768]{3,2,1,0:T(8,128)(2,1)}, u32[]{:S(2)}, u32[]{:S(2)}) collective-permute-start(bf16[2,3,48,768]{3,2,1,0:T(8,128)(2,1)S(1)} %pad_maximum_fusion.1.rest_10_.rest_0_), channel_id=1, source_target_pairs={{0,8},{2,10},{4,12},{6,14},{8,0},{10,2},{12,4},{14,6},{16,24},{18,... | collective-permute-start | bytes 1327112 | tf_op jit(solution)/shard_map/ppermute | solution.py:697
  72.5 19.8 %collective-permute-start.29 = (bf16[2,3,48,768]{3,2,1,0:T(8,128)(2,1)S(1)}, bf16[2,3,48,768]{3,2,1,0:T(8,128)(2,1)S(1)}, u32[]{:S(2)}, u32[]{:S(2)}) collective-permute-start(bf16[2,3,48,768]{3,2,1,0:T(8,128)(2,1)S(1)} %collective-permute-done.24.rest_5_), channel_id=1, source_target_pairs={{0,4},{2,6},{4,0},{6,2},{8,12},{10,14},{12,8},{14,10},{16,20},{18,... | collective-permute-start | bytes 1327112 | tf_op jit(solution)/shard_map/ppermute | solution.py:697
  94.0 21.5 %collective-permute-start.33 = (bf16[2,3,48,768]{3,2,1,0:T(8,128)(2,1)}, bf16[2,3,48,768]{3,2,1,0:T(8,128)(2,1)S(1)}, u32[]{:S(2)}, u32[]{:S(2)}) collective-permute-start(bf16[2,3,48,768]{3,2,1,0:T(8,128)(2,1)} %collective-permute-done.31.rest_11_.rest_1_), channel_id=1, source_target_pairs={{0,4},{2,6},{4,0},{6,2},{8,12},{10,14},{12,8},{14,10},{16,20},{18,... | collective-permute-start | bytes 1327112 | tf_op jit(solution)/shard_map/ppermute | solution.py:697
  129.8 20.9 %collective-permute-start.37 = (bf16[4,3,48,768]{3,2,1,0:T(8,128)(2,1)}, bf16[4,3,48,768]{3,2,1,0:T(8,128)(2,1)S(1)}, u32[]{:S(2)}, u32[]{:S(2)}) collective-permute-start(bf16[4,3,48,768]{3,2,1,0:T(8,128)(2,1)} %get-tuple-element.150), channel_id=1, source_target_pairs={{0,4},{2,6},{4,0},{6,2},{8,12},{10,14},{12,8},{14,10},{16,20},{18,... | collective-permute-start | bytes 2654216 | tf_op jit(solution)/shard_map/ppermute | solution.py:697
  155.2 30.3 %collective-permute-start.40 = (bf16[3,272,768]{2,1,0:T(8,128)(2,1)S(1)}, bf16[3,272,768]{2,1,0:T(8,128)(2,1)S(1)}, u32[]{:S(2)}, u32[]{:S(2)}) collective-permute-start(bf16[3,272,768]{2,1,0:T(8,128)(2,1)S(1)} %add_convert_fusion.1.dm_ref), channel_id=1, source_target_pairs={{0,1},{1,0},{2,3},{3,2},{4,5},{5,4},{6,7},{7,6},{8,9},{9,8},{10,11... | collective-permute-start | bytes 3760136 | tf_op jit(solution)/shard_map/ppermute | solution.py:725
  156.7 28.7 %collective-permute-start.41 = (bf16[4,3,48,768]{3,2,1,0:T(8,128)(2,1)}, bf16[4,3,48,768]{3,2,1,0:T(8,128)(2,1)}, u32[]{:S(2)}, u32[]{:S(2)}) collective-permute-start(bf16[4,3,48,768]{3,2,1,0:T(8,128)(2,1)} %get-tuple-element.167), channel_id=1, source_target_pairs={{0,4},{2,6},{4,0},{6,2},{8,12},{10,14},{12,8},{14,10},{16,20},{18,... | collective-permute-start | bytes 2654216 | tf_op jit(solution)/shard_map/ppermute | solution.py:697
  191.3 31.6 %collective-permute-start.44 = (bf16[3,272,768]{2,1,0:T(8,128)(2,1)S(1)}, bf16[3,272,768]{2,1,0:T(8,128)(2,1)}, u32[]{:S(2)}, u32[]{:S(2)}) collective-permute-start(bf16[3,272,768]{2,1,0:T(8,128)(2,1)S(1)} %add_convert_fusion.zm_ref), channel_id=1, source_target_pairs={{0,1},{1,0},{2,3},{3,2},{4,5},{5,4},{6,7},{7,6},{8,9},{9,8},{10,11... | collective-permute-start | bytes 3760136 | tf_op jit(solution)/shard_map/ppermute | solution.py:725
  192.3 30.6 %collective-permute-start.45 = (bf16[4,3,48,768]{3,2,1,0:T(8,128)(2,1)}, bf16[4,3,48,768]{3,2,1,0:T(8,128)(2,1)}, u32[]{:S(2)}, u32[]{:S(2)}) collective-permute-start(bf16[4,3,48,768]{3,2,1,0:T(8,128)(2,1)} %get-tuple-element.181), channel_id=1, source_target_pairs={{0,4},{2,6},{4,0},{6,2},{8,12},{10,14},{12,8},{14,10},{16,20},{18,... | collective-permute-start | bytes 2654216 | tf_op jit(solution)/shard_map/ppermute | solution.py:697
  193.6 31.6 %collective-permute-start.46 = (bf16[2,3,48,768]{3,2,1,0:T(8,128)(2,1)}, bf16[2,3,48,768]{3,2,1,0:T(8,128)(2,1)}, u32[]{:S(2)}, u32[]{:S(2)}) collective-permute-start(bf16[2,3,48,768]{3,2,1,0:T(8,128)(2,1)} %add_convert_fusion.6), channel_id=1, source_target_pairs={{0,8},{2,10},{4,12},{6,14},{8,0},{10,2},{12,4},{14,6},{16,24},{18,... | collective-permute-start | bytes 1327112 | tf_op jit(solution)/shard_map/ppermute | solution.py:697
  195.3 37.8 %collective-permute-start.48 = (bf16[4,3,48,768]{3,2,1,0:T(8,128)(2,1)}, bf16[4,3,48,768]{3,2,1,0:T(8,128)(2,1)}, u32[]{:S(2)}, u32[]{:S(2)}) collective-permute-start(bf16[4,3,48,768]{3,2,1,0:T(8,128)(2,1)} %get-tuple-element.187), channel_id=1, source_target_pairs={{0,4},{2,6},{4,0},{6,2},{8,12},{10,14},{12,8},{14,10},{16,20},{18,... | collective-permute-start | bytes 2654216 | tf_op jit(solution)/shard_map/ppermute | solution.py:697
  228.5 18.0 %collective-permute-start.54 = (bf16[3,48,768]{2,1,0:T(8,128)(2,1)}, bf16[3,48,768]{2,1,0:T(8,128)(2,1)}, u32[]{:S(2)}, u32[]{:S(2)}) collective-permute-start(bf16[3,48,768]{2,1,0:T(8,128)(2,1)} %fusion.2), channel_id=1, source_target_pairs={{0,16},{2,18},{4,20},{6,22},{8,24},{10,26},{12,28},{14,30},{16,0},... | collective-permute-start | bytes 663560 | tf_op jit(solution)/shard_map/ppermute | solution.py:697
  233.0 17.5 %collective-permute-start.53 = (bf16[2,3,48,768]{3,2,1,0:T(8,128)(2,1)}, bf16[2,3,48,768]{3,2,1,0:T(8,128)(2,1)}, u32[]{:S(2)}, u32[]{:S(2)}) collective-permute-start(bf16[2,3,48,768]{3,2,1,0:T(8,128)(2,1)} %add_convert_fusion.5), channel_id=1, source_target_pairs={{0,8},{2,10},{4,12},{6,14},{8,0},{10,2},{12,4},{14,6},{16,24},{18,... | collective-permute-start | bytes 1327112 | tf_op jit(solution)/shard_map/ppermute | solution.py:697
  234.7 35.1 %collective-permute-start.51 = (bf16[3,272,768]{2,1,0:T(8,128)(2,1)S(1)}, bf16[3,272,768]{2,1,0:T(8,128)(2,1)}, u32[]{:S(2)}, u32[]{:S(2)}) collective-permute-start(bf16[3,272,768]{2,1,0:T(8,128)(2,1)S(1)} %copy-done.19), channel_id=1, source_target_pairs={{0,1},{1,0},{2,3},{3,2},{4,5},{5,4},{6,7},{7,6},{8,9},{9,8},{10,11... | collective-permute-start | bytes 3760136 | tf_op jit(solution)/shard_map/ppermute | solution.py:725
  240.5 17.4 %collective-permute-start.56 = (bf16[2,3,48,768]{3,2,1,0:T(8,128)(2,1)}, bf16[2,3,48,768]{3,2,1,0:T(8,128)(2,1)S(1)}, u32[]{:S(2)}, u32[]{:S(2)}) collective-permute-start(bf16[2,3,48,768]{3,2,1,0:T(8,128)(2,1)} %add_convert_fusion.4), channel_id=1, source_target_pairs={{0,8},{2,10},{4,12},{6,14},{8,0},{10,2},{12,4},{14,6},{16,24},{18,... | collective-permute-start | bytes 1327112 | tf_op jit(solution)/shard_map/ppermute | solution.py:697
  246.5 23.3 %collective-permute-start.57 = (bf16[4,4,48,384]{3,2,1,0:T(8,128)(2,1)S(1)}, bf16[4,4,48,384]{3,2,1,0:T(8,128)(2,1)S(1)}, u32[]{:S(2)}, u32[]{:S(2)}) collective-permute-start(bf16[4,4,48,384]{3,2,1,0:T(8,128)(2,1)S(1)} %copy-done.36), channel_id=1, source_target_pairs={{0,4},{2,6},{4,0},{6,2},{8,12},{10,14},{12,8},{14,10},{16,20},{18,... | collective-permute-start | bytes 1769480 | tf_op jit(solution)/shard_map/ppermute | solution.py:697
  253.8 26.3 %collective-permute-start.59 = (bf16[3,48,768]{2,1,0:T(8,128)(2,1)}, bf16[3,48,768]{2,1,0:T(8,128)(2,1)}, u32[]{:S(2)}, u32[]{:S(2)}) collective-permute-start(bf16[3,48,768]{2,1,0:T(8,128)(2,1)} %fusion.3), channel_id=1, source_target_pairs={{0,16},{2,18},{4,20},{6,22},{8,24},{10,26},{12,28},{14,30},{16,0},... | collective-permute-start | bytes 663560 | tf_op jit(solution)/shard_map/ppermute | solution.py:697
  269.6 18.5 %collective-permute-start.62 = (bf16[3,48,768]{2,1,0:T(8,128)(2,1)}, bf16[3,48,768]{2,1,0:T(8,128)(2,1)}, u32[]{:S(2)}, u32[]{:S(2)}) collective-permute-start(bf16[3,48,768]{2,1,0:T(8,128)(2,1)} %fusion.4), channel_id=1, source_target_pairs={{0,16},{2,18},{4,20},{6,22},{8,24},{10,26},{12,28},{14,30},{16,0},... | collective-permute-start | bytes 663560 | tf_op jit(solution)/shard_map/ppermute | solution.py:697
  (115 other events, 1191.1 us)

commit v2 on v1

--- a/solution.py
+++ b/solution.py
@@ -755,8 +755,8 @@
         rel = [0, 4, 8, 12]
         rel = rel + [r ^ 2 for r in rel]
         attn_off = (here ^ jnp.array(rel + [r ^ 1 for r in rel], jnp.int32)) * share
-        rel = [r ^ j for r in rel for j in (0, 1)]
-        ffn_off = (here ^ jnp.array(rel, jnp.int32)) * share
+        rel = jnp.array([r ^ j for r in rel for j in (0, 1)], jnp.int32)
+        ffn_off = (here ^ rel) * share
         mine, other = halves(w_up)
         up_own = jnp.stack([mine, partner(other)])
         mine, other = halves(w_down)
@@ -827,7 +827,7 @@
     act, slope = experts_up(tie(experts_two, *stage), ffn_off, b_two, b_up_mine, up_pieces)
     stage = [act]
     if by_permute:
-        stage = stage + [x1d, z12d, x2d]
+        stage = stage + [x1d, z12d]
         x3d = dp_swap(tie(z12d, *stage), 2)
     *down_grad, grad_b_down = weight_grad(
         tie(experts_two, *stage), slots, 0, cots, act, ffn_chunk, n_out, e_count, items
@@ -860,7 +860,8 @@
                 + end[planes].astype(F32)
             )
 
-        stage = stage + [x3d]
+        ffn_off = (tie(here, x2d, *stage) ^ rel) * share
+        stage = stage + [tie(x3d, ffn_off)]
         dn1 = near(down_grad, 1, *stage)
     db_own, db_other, du, grad_b_up = experts_back(
         tie(experts_two, *stage), ffn_off, cots, slope, up_pieces, down_pieces, items

time: 301 us -> 296 us (0.983)
  starting transfers between devices: 53.7 us -> 50.1 us
    ppermute x60, starting transfers between devices: 48.2 us -> 44 us  [swap(): return lax.ppermute(value, axis, [(i, i ^ mask) for i in range(size)])]
  transfers between devices with their start and end apart: 66 -> 66, of which waited for: 23 -> 24; matrix products, arithmetic and copies ran while one was open for 14% -> 15% of each run, Pallas kernels for 41% -> 42%
where the time goes in v2:
time: 296 us; the launch traced here: 295 us
  Pallas kernels  123 us (42%)
  waiting for transfers between devices  65.7 us (22%)
  starting transfers between devices  50.1 us (17%)
  other arithmetic  34.8 us (12%)
  local copies, waits for them, and re-layouts  19.2 us (6%)
    ppermute x60, waiting for transfers between devices, swap(): return lax.ppermute(value, axis, [(i, i ^ mask) for i in range(size)])  62.7 us
    ppermute x60, starting transfers between devices, swap(): return lax.ppermute(value, axis, [(i, i ^ mask) for i in range(size)])  44 us
    pallas_call x1, Pallas kernels, attend_back(): pl.pallas_call(functools.partial(k_attend_back, scale=scale), grid_spec=g...  26.8 us
    pallas_call x2, Pallas kernels, weight_grad(): pl.pallas_call(functools.partial(k_weight_grad, n_left=len(left), n_out=n...  26.4 us
    pallas_call x1, Pallas kernels, experts_back(): pl.pallas_call(functools.partial(k_back, n_left=len(left), n_up=len(ups),...  15.9 us
    pallas_call x1, Pallas kernels, experts_down(): pl.pallas_call(functools.partial(k_down, own=own), grid_spec=grid_spec, o...  10.8 us
    pallas_call x1, Pallas kernels, experts_up(): pl.pallas_call(functools.partial(k_up, n_left=len(b)), grid_spec=grid_spe...  10.2 us
    pallas_call x1, Pallas kernels, project(): pl.pallas_call(k_proj, grid_spec=grid_spec, out_shape=[jax.ShapeDtypeStru...  8.75 us
  transfers between devices with their start and end apart: 66, of which 24 were waited for; matrix products, arithmetic and copies ran while one was open for 15% of the time, Pallas kernels for 42%

profile of v2, /device:TPU:0, one launch (start us, length us, event | category | flops | bytes accessed | tf_op | source)
XLA Modules:
  0.0 294.6 jit_solution(4999579260823860036)
XLA Ops:
  2.2 3.8 %collective-permute-start.2 = (bf16[1,4,48,384]{3,2,1,0:T(8,128)(2,1)S(1)}, bf16[1,4,48,384]{3,2,1,0:T(8,128)(2,1)S(1)}, u32[]{:S(2)}, u32[]{:S(2)}) collective-permute-start(bf16[1,4,48,384]{3,2,1,0:T(8,128)(2,1)S(1)} %maximum_bitcast_fusion.rest_0_), channel_id=1, source_target_pairs={{0,16},{2,18},{4,20},{6,22},{8,24},{10,26},{12,28},{14,30},{16,0},... | collective-permute-start | bytes 442376 | tf_op jit(solution)/shard_map/ppermute | solution.py:697
  10.3 3.4 %collective-permute-done.2.rest_2_ = bf16[1,4,48,384]{3,2,1,0:T(8,128)(2,1)S(1)} collective-permute-done((bf16[1,4,48,384]{3,2,1,0:T(8,128)(2,1)S(1)}, bf16[1,4,48,384]{3,2,1,0:T(8,128)(2,1)S(1)}, u32[]{:S(2)}, u32[]{:S(2)}) %collective-permute-start.2) | collective-permute-done | bytes 147488 | tf_op jit(solution)/shard_map/ppermute | solution.py:697
  36.2 8.8 %project.1 = (bf16[3,272,768]{2,1,0:T(8,128)(2,1)}, bf16[3,3,272,384]{3,2,1,0:T(8,128)(2,1)}, bf16[3,768,384]{2,1,0:T(8,128)(2,1)}, bf16[1,768,384]{2,1,0:T(8,128)(2,1)}) custom-call(s32[16]{0:T(128)} %xor_multiply_fusion.2.off_ref, bf16[3,272,768]{2,1,0:T(8,128)(2,1)} %pad.10.tok_ref, f32[5,768]{1,0:T(8,128)} %stack.48.vec_ref, ...), custom_call_target="tpu_custom_call" | custom-call | flops 1 | bytes 1 | tf_op jit(solution)/shard_map/project/pallas_call | solution.py:138
  44.9 5.7 %collective-permute-done.17.rest_3_ = bf16[2,3,48,768]{3,2,1,0:T(8,128)(2,1)S(1)} collective-permute-done((bf16[2,3,48,768]{3,2,1,0:T(8,128)(2,1)S(1)}, bf16[2,3,48,768]{3,2,1,0:T(8,128)(2,1)S(1)}, u32[]{:S(2)}, u32[]{:S(2)}) %collective-permute-start.17) | collective-permute-done | bytes 442400 | tf_op jit(solution)/shard_map/ppermute | solution.py:697
  59.1 8.3 %attend.1.cm_ref.c_ref = bf16[3,272,384]{2,1,0:T(8,128)(2,1)} custom-call(s32[3]{0:T(128)} %len_ref.1, bf16[3,3,272,384]{3,2,1,0:T(8,128)(2,1)} %get-tuple-element.128.q_ref.k_ref.v_ref, bf16[3,3,272,384]{3,2,1,0:T(8,128)(2,1)} %get-tuple-element.128.q_ref.k_ref.v_ref, bf16[3,3,272,384]{3,2,1,0:T(8,128)(2,1)} %get-tuple-element.128.q_ref.k_ref.v_ref), custom_call_target="tpu_custom_call" | custom-call | flops 1 | bytes 1 | tf_op jit(solution)/shard_map/attend/pallas_call | solution.py:183
  77.8 3.8 %collective-permute-done.28.rest_8_ = bf16[2,3,48,768]{3,2,1,0:T(8,128)(2,1)S(1)} collective-permute-done((bf16[2,3,48,768]{3,2,1,0:T(8,128)(2,1)S(1)}, bf16[2,3,48,768]{3,2,1,0:T(8,128)(2,1)S(1)}, u32[]{:S(2)}, u32[]{:S(2)}) %collective-permute-start.28) | collective-permute-done | bytes 442400 | tf_op jit(solution)/shard_map/ppermute | solution.py:697
  85.2 5.5 %residual.1 = (f32[3,272,768]{2,1,0:T(8,128)}, bf16[3,272,768]{2,1,0:T(8,128)(2,1)}) custom-call(bf16[3,272,768]{2,1,0:T(8,128)(2,1)} %pad.10.tok_ref, bf16[3,272,384]{2,1,0:T(8,128)(2,1)} %attend.1.cm_ref.c_ref, bf16[3,272,384]{2,1,0:T(8,128)(2,1)} %copy-done.33, bf16[1,768,384]{2,1,0:T(8,128)(2,1)} %get-tuple-element.122.wm_ref.wo_ref, ...), custom_call_target="tpu_custom_call" | custom-call | flops 1 | bytes 1 | tf_op jit(solution)/shard_map/residual/pallas_call | solution.py:204
  98.3 10.2 %experts_up.1 = (bf16[6,288,768]{2,1,0:T(8,128)(2,1)}, bf16[6,288,768]{2,1,0:T(8,128)(2,1)}) custom-call(s32[2,6]{1,0:T(2,128)} %pad_add_fusion.1.e_ref, s32[16]{0:T(128)} %xor_multiply_fusion.1.off_ref, f32[3,768]{1,0:T(4,128)} %constant_dynamic-slice_fusion.bias_ref, bf16[3,272,768]{2,1,0:T(8,128)(2,1)} %get-tuple-element.143.rest_0_, ...), custom_call_target="tpu_custom_call" | custom-call | flops 1 | bytes 1 | tf_op jit(solution)/shard_map/experts_up/pallas_call | solution.py:328
  109.6 13.2 %weight_grad.2 = (bf16[4,3,48,768]{3,2,1,0:T(8,128)(2,1)}, bf16[4,3,48,768]{3,2,1,0:T(8,128)(2,1)}, bf16[4,3,48,768]{3,2,1,0:T(8,128)(2,1)}, bf16[4,3,48,768]{3,2,1,0:T(8,128)(2,1)}, f32[3,768]{1,0:T(4,128)}) custom-call(s32[2,6]{1,0:T(2,128)} %pad_add_fusion.1.e_ref, s32[16]{0:T(128)} %fusion.6.slot_ref, ...), custom_call_target="tpu_custom_call" | custom-call | flops 1 | bytes 1 | tf_op jit(solution)/shard_map/weight_grad/pallas_call | solution.py:387
  125.7 15.9 %experts_back.1 = (bf16[3,272,768]{2,1,0:T(8,128)(2,1)}, bf16[3,272,768]{2,1,0:T(8,128)(2,1)}, bf16[6,288,768]{2,1,0:T(8,128)(2,1)}, f32[3,768]{1,0:T(4,128)}) custom-call(s32[2,6]{1,0:T(2,128)} %pad_add_fusion.1.e_ref, s32[16]{0:T(128)} %xor_multiply_fusion.off_ref, bf16[6,288,768]{2,1,0:T(8,128)(2,1)} %get-tuple-element.156.slope_ref, ...), custom_call_target="tpu_custom_call" | custom-call | flops 1 | bytes 1 | tf_op jit(solution)/shard_map/experts_back/pallas_call | solution.py:474
  141.6 4.5 %collective-permute-done.37 = bf16[4,3,48,768]{3,2,1,0:T(8,128)(2,1)S(1)} collective-permute-done((bf16[4,3,48,768]{3,2,1,0:T(8,128)(2,1)}, bf16[4,3,48,768]{3,2,1,0:T(8,128)(2,1)S(1)}, u32[]{:S(2)}, u32[]{:S(2)}) %collective-permute-start.37) | collective-permute-done | bytes 884768 | tf_op jit(solution)/shard_map/ppermute | solution.py:697
  147.0 3.2 %collective-permute-done.38 = bf16[3,272,768]{2,1,0:T(8,128)(2,1)S(1)} collective-permute-done((bf16[3,272,768]{2,1,0:T(8,128)(2,1)}, bf16[3,272,768]{2,1,0:T(8,128)(2,1)S(1)}, u32[]{:S(2)}, u32[]{:S(2)}) %collective-permute-start.38) | collective-permute-done | bytes 1253408 | tf_op jit(solution)/shard_map/ppermute | solution.py:697
  154.3 13.2 %weight_grad.3 = (bf16[4,3,48,768]{3,2,1,0:T(8,128)(2,1)}, bf16[4,3,48,768]{3,2,1,0:T(8,128)(2,1)}, bf16[4,3,48,768]{3,2,1,0:T(8,128)(2,1)}, bf16[4,3,48,768]{3,2,1,0:T(8,128)(2,1)}, f32[3,768]{1,0:T(4,128)}) custom-call(s32[2,6]{1,0:T(2,128)} %pad_add_fusion.1.e_ref, s32[16]{0:T(128)} %fusion.6.slot_ref, bf16[6,288,768]{2,1,0:T(8,128)(2,1)} %get-tuple-element.157.right_ref, ...), custom_call_target="tpu_custom_call" | custom-call | flops 1 | bytes 1 | tf_op jit(solution)/shard_map/weight_grad/pallas_call | solution.py:387
  169.2 10.8 %experts_down.1 = (bf16[3,272,768]{2,1,0:T(8,128)(2,1)}, bf16[3,272,768]{2,1,0:T(8,128)(2,1)}) custom-call(s32[2,6]{1,0:T(2,128)} %pad_add_fusion.1.e_ref, s32[16]{0:T(128)} %xor_multiply_fusion.off_ref, bf16[6,288,768]{2,1,0:T(8,128)(2,1)} %get-tuple-element.144.right_ref.act_ref, bf16[2,3,48,768]{3,2,1,0:T(8,128)(2,1)} %copy-done.6, ...), custom_call_target="tpu_custom_call" | custom-call | flops 1 | bytes 1 | tf_op jit(solution)/shard_map/experts_down/pallas_call | solution.py:529
  182.6 3.2 %collective-permute-done.43 = bf16[3,272,768]{2,1,0:T(8,128)(2,1)S(1)} collective-permute-done((bf16[3,272,768]{2,1,0:T(8,128)(2,1)}, bf16[3,272,768]{2,1,0:T(8,128)(2,1)S(1)}, u32[]{:S(2)}, u32[]{:S(2)}) %collective-permute-start.43) | collective-permute-done | bytes 1253408 | tf_op jit(solution)/shard_map/ppermute | solution.py:697
  191.2 26.8 %attend_back.1 = (f32[3,272,768]{2,1,0:T(8,128)}, bf16[3,272,768]{2,1,0:T(8,128)(2,1)}, f32[2,768]{1,0:T(2,128)}, f32[3,768]{1,0:T(4,128)}, f32[2,384]{1,0:T(2,1...) custom-call(s32[3]{0:T(128)} %len_ref.1, ...), custom_call_target="tpu_custom_call" | custom-call | flops 1 | bytes 1 | tf_op jit(solution)/shard_map/attend_back/pallas_call | solution.py:657
  224.9 3.2 %collective-permute-done.48 = bf16[4,3,48,768]{3,2,1,0:T(8,128)(2,1)} collective-permute-done((bf16[4,3,48,768]{3,2,1,0:T(8,128)(2,1)}, bf16[4,3,48,768]{3,2,1,0:T(8,128)(2,1)}, u32[]{:S(2)}, u32[]{:S(2)}) %collective-permute-start.48) | collective-permute-done | bytes 884768 | tf_op jit(solution)/shard_map/ppermute | solution.py:697
  236.4 4.9 %finish_output.1 = bf16[3,261,768]{2,1,0:T(8,128)(2,1)} custom-call(s32[2,3]{1,0:T(2,128)} %copy-done.68, f32[3,272,768]{2,1,0:T(8,128)} %get-tuple-element.138.h_ref, bf16[3,272,768]{2,1,0:T(8,128)(2,1)} %copy-done.2, bf16[3,272,768]{2,1,0:T(8,128)(2,1)} %collective-permute-done.44.zp_ref, f32[3,768]{1,0:T(4,128)} %bias_ref.1), custom_call_target="tpu_custom_call" | custom-call | flops 1 | bytes 1 | tf_op jit(solution)/shard_map/finish_output/pallas_call | solution.py:559
  242.5 3.6 %collective-permute-done.53 = bf16[2,3,48,768]{3,2,1,0:T(8,128)(2,1)} collective-permute-done((bf16[2,3,48,768]{3,2,1,0:T(8,128)(2,1)}, bf16[2,3,48,768]{3,2,1,0:T(8,128)(2,1)}, u32[]{:S(2)}, u32[]{:S(2)}) %collective-permute-start.53) | collective-permute-done | bytes 442400 | tf_op jit(solution)/shard_map/ppermute | solution.py:697
  249.6 3.9 %collective-permute-done.56 = bf16[2,3,48,768]{3,2,1,0:T(8,128)(2,1)S(1)} collective-permute-done((bf16[2,3,48,768]{3,2,1,0:T(8,128)(2,1)}, bf16[2,3,48,768]{3,2,1,0:T(8,128)(2,1)S(1)}, u32[]{:S(2)}, u32[]{:S(2)}) %collective-permute-start.56) | collective-permute-done | bytes 442400 | tf_op jit(solution)/shard_map/ppermute | solution.py:697
  255.4 8.8 %collective-permute-done.55 = f32[15,768]{1,0:T(8,128)S(1)} collective-permute-done((f32[15,768]{1,0:T(8,128)S(1)}, f32[15,768]{1,0:T(8,128)S(1)}, u32[]{:S(2)}, u32[]{:S(2)}) %collective-permute-start.55) | collective-permute-done | bytes 46112 | tf_op jit(solution)/shard_map/ppermute | solution.py:697
  269.5 5.7 %token_grad.1 = f32[3,261,768]{2,1,0:T(8,128)} custom-call(f32[3,272,768]{2,1,0:T(8,128)} %get-tuple-element.205.dh_ref, bf16[3,272,768]{2,1,0:T(8,128)(2,1)} %get-tuple-element.207.dm_ref, bf16[3,272,768]{2,1,0:T(8,128)(2,1)} %collective-permute-done.51.dp_ref, bf16[3,272,768]{2,1,0:T(8,128)(2,1)} %pad.10.tok_ref, f32[5,768]{1,0:T(8,128)} %stack.48.vec_ref), custom_call_target="tpu_custom_call" | custom-call | flops 1 | bytes 1 | tf_op jit(solution)/shard_map/token_grad/pallas_call | solution.py:684
  277.7 3.1 %collective-permute-done.64 = f32[15,768]{1,0:T(8,128)S(1)} collective-permute-done((f32[15,768]{1,0:T(8,128)S(1)}, f32[15,768]{1,0:T(8,128)S(1)}, u32[]{:S(2)}, u32[]{:S(2)}) %collective-permute-start.64) | collective-permute-done | bytes 46112 | tf_op jit(solution)/shard_map/ppermute | solution.py:697
  282.9 3.1 %collective-permute-done.65 = f32[15,768]{1,0:T(8,128)S(1)} collective-permute-done((f32[15,768]{1,0:T(8,128)S(1)}, f32[15,768]{1,0:T(8,128)S(1)}, u32[]{:S(2)}, u32[]{:S(2)}) %collective-permute-start.65) | collective-permute-done | bytes 46112 | tf_op jit(solution)/shard_map/ppermute | solution.py:697
  (332 shorter events, 116.4 us)
Async XLA Ops:
  0.7 33.4 %collective-permute-start = (bf16[3,261,768]{2,1,0:T(8,128)(2,1)}, bf16[3,261,768]{2,1,0:T(8,128)(2,1)}, u32[]{:S(2)}, u32[]{:S(2)}) collective-permute-start(bf16[3,261,768]{2,1,0:T(8,128)(2,1)} %param.33), channel_id=1, source_target_pairs={{0,2},{2,0},{4,6},{6,4},{8,10},{10,8},{12,14},{14,12},{16,18},{18,... | collective-permute-start | bytes 3608072 | tf_op jit(solution)/shard_map/ppermute | solution.py:697
  28.5 22.1 %collective-permute-start.17 = (bf16[2,3,48,768]{3,2,1,0:T(8,128)(2,1)S(1)}, bf16[2,3,48,768]{3,2,1,0:T(8,128)(2,1)S(1)}, u32[]{:S(2)}, u32[]{:S(2)}) collective-permute-start(bf16[2,3,48,768]{3,2,1,0:T(8,128)(2,1)S(1)} %pad_maximum_fusion.rest_2_), channel_id=1, source_target_pairs={{0,8},{2,10},{4,12},{6,14},{8,0},{10,2},{12,4},{14,6},{16,24},{18,... | collective-permute-start | bytes 1327112 | tf_op jit(solution)/shard_map/ppermute | solution.py:697
  29.4 21.2 %collective-permute-start.18 = (bf16[2,3,48,768]{3,2,1,0:T(8,128)(2,1)S(1)}, bf16[2,3,48,768]{3,2,1,0:T(8,128)(2,1)S(1)}, u32[]{:S(2)}, u32[]{:S(2)}) collective-permute-start(bf16[2,3,48,768]{3,2,1,0:T(8,128)(2,1)S(1)} %pad_maximum_fusion.rest_2_), channel_id=1, source_target_pairs={{0,16},{2,18},{4,20},{6,22},{8,24},{10,26},{12,28},{14,30},{16,0},... | collective-permute-start | bytes 1327112 | tf_op jit(solution)/shard_map/ppermute | solution.py:697
  31.4 19.2 %collective-permute-start.19 = (bf16[2,3,48,768]{3,2,1,0:T(8,128)(2,1)S(1)}, bf16[2,3,48,768]{3,2,1,0:T(8,128)(2,1)S(1)}, u32[]{:S(2)}, u32[]{:S(2)}) collective-permute-start(bf16[2,3,48,768]{3,2,1,0:T(8,128)(2,1)S(1)} %pad_maximum_fusion.rest_2_), channel_id=1, source_target_pairs={{0,4},{2,6},{4,0},{6,2},{8,12},{10,14},{12,8},{14,10},{16,20},{18,... | collective-permute-start | bytes 1327112 | tf_op jit(solution)/shard_map/ppermute | solution.py:697
  32.3 20.8 %collective-permute-start.21 = (bf16[2,3,48,768]{3,2,1,0:T(8,128)(2,1)S(1)}, bf16[2,3,48,768]{3,2,1,0:T(8,128)(2,1)S(1)}, u32[]{:S(2)}, u32[]{:S(2)}) collective-permute-start(bf16[2,3,48,768]{3,2,1,0:T(8,128)(2,1)S(1)} %pad_maximum_fusion.1.rest_10_.rest_0_), channel_id=1, source_target_pairs={{0,4},{2,6},{4,0},{6,2},{8,12},{10,14},{12,8},{14,10},{16,20},{18,... | collective-permute-start | bytes 1327112 | tf_op jit(solution)/shard_map/ppermute | solution.py:697
  70.0 22.1 %collective-permute-start.30 = (bf16[2,3,48,768]{3,2,1,0:T(8,128)(2,1)S(1)}, bf16[2,3,48,768]{3,2,1,0:T(8,128)(2,1)}, u32[]{:S(2)}, u32[]{:S(2)}) collective-permute-start(bf16[2,3,48,768]{3,2,1,0:T(8,128)(2,1)S(1)} %pad_maximum_fusion.1.rest_10_.rest_0_), channel_id=1, source_target_pairs={{0,16},{2,18},{4,20},{6,22},{8,24},{10,26},{12,28},{14,30},{16,0},... | collective-permute-start | bytes 1327112 | tf_op jit(solution)/shard_map/ppermute | solution.py:697
  71.4 20.9 %collective-permute-start.31 = (bf16[2,3,48,768]{3,2,1,0:T(8,128)(2,1)S(1)}, bf16[2,3,48,768]{3,2,1,0:T(8,128)(2,1)}, u32[]{:S(2)}, u32[]{:S(2)}) collective-permute-start(bf16[2,3,48,768]{3,2,1,0:T(8,128)(2,1)S(1)} %pad_maximum_fusion.1.rest_10_.rest_0_), channel_id=1, source_target_pairs={{0,8},{2,10},{4,12},{6,14},{8,0},{10,2},{12,4},{14,6},{16,24},{18,... | collective-permute-start | bytes 1327112 | tf_op jit(solution)/shard_map/ppermute | solution.py:697
  72.5 19.8 %collective-permute-start.29 = (bf16[2,3,48,768]{3,2,1,0:T(8,128)(2,1)S(1)}, bf16[2,3,48,768]{3,2,1,0:T(8,128)(2,1)S(1)}, u32[]{:S(2)}, u32[]{:S(2)}) collective-permute-start(bf16[2,3,48,768]{3,2,1,0:T(8,128)(2,1)S(1)} %collective-permute-done.24.rest_5_), channel_id=1, source_target_pairs={{0,4},{2,6},{4,0},{6,2},{8,12},{10,14},{12,8},{14,10},{16,20},{18,... | collective-permute-start | bytes 1327112 | tf_op jit(solution)/shard_map/ppermute | solution.py:697
  94.5 28.4 %collective-permute-start.36 = (bf16[2,3,48,768]{3,2,1,0:T(8,128)(2,1)}, bf16[2,3,48,768]{3,2,1,0:T(8,128)(2,1)S(1)}, u32[]{:S(2)}, u32[]{:S(2)}) collective-permute-start(bf16[2,3,48,768]{3,2,1,0:T(8,128)(2,1)} %collective-permute-done.30.rest_12_.rest_2_), channel_id=1, source_target_pairs={{0,4},{2,6},{4,0},{6,2},{8,12},{10,14},{12,8},{14,10},{16,20},{18,... | collective-permute-start | bytes 1327112 | tf_op jit(solution)/shard_map/ppermute | solution.py:697
  108.5 16.4 %collective-permute-start.35 = (bf16[2,3,48,768]{3,2,1,0:T(8,128)(2,1)S(1)}, bf16[2,3,48,768]{3,2,1,0:T(8,128)(2,1)S(1)}, u32[]{:S(2)}, u32[]{:S(2)}) collective-permute-start(bf16[2,3,48,768]{3,2,1,0:T(8,128)(2,1)S(1)} %collective-permute-done.34.rest_13_.rest_3_), channel_id=1, source_target_pairs={{0,4},{2,6},{4,0},{6,2},{8,12},{10,14},{12,8},{14,10},{16,20},{18,... | collective-permute-start | bytes 1327112 | tf_op jit(solution)/shard_map/ppermute | solution.py:697
  124.9 21.1 %collective-permute-start.37 = (bf16[4,3,48,768]{3,2,1,0:T(8,128)(2,1)}, bf16[4,3,48,768]{3,2,1,0:T(8,128)(2,1)S(1)}, u32[]{:S(2)}, u32[]{:S(2)}) collective-permute-start(bf16[4,3,48,768]{3,2,1,0:T(8,128)(2,1)} %get-tuple-element.154), channel_id=1, source_target_pairs={{0,4},{2,6},{4,0},{6,2},{8,12},{10,14},{12,8},{14,10},{16,20},{18,... | collective-permute-start | bytes 2654216 | tf_op jit(solution)/shard_map/ppermute | solution.py:697
  150.5 29.7 %collective-permute-start.40 = (bf16[3,272,768]{2,1,0:T(8,128)(2,1)S(1)}, bf16[3,272,768]{2,1,0:T(8,128)(2,1)S(1)}, u32[]{:S(2)}, u32[]{:S(2)}) collective-permute-start(bf16[3,272,768]{2,1,0:T(8,128)(2,1)S(1)} %add_convert_fusion.1.dm_ref), channel_id=1, source_target_pairs={{0,1},{1,0},{2,3},{3,2},{4,5},{5,4},{6,7},{7,6},{8,9},{9,8},{10,11... | collective-permute-start | bytes 3760136 | tf_op jit(solution)/shard_map/ppermute | solution.py:725
  152.1 27.9 %collective-permute-start.41 = (bf16[4,3,48,768]{3,2,1,0:T(8,128)(2,1)}, bf16[4,3,48,768]{3,2,1,0:T(8,128)(2,1)}, u32[]{:S(2)}, u32[]{:S(2)}) collective-permute-start(bf16[4,3,48,768]{3,2,1,0:T(8,128)(2,1)} %get-tuple-element.171), channel_id=1, source_target_pairs={{0,4},{2,6},{4,0},{6,2},{8,12},{10,14},{12,8},{14,10},{16,20},{18,... | collective-permute-start | bytes 2654216 | tf_op jit(solution)/shard_map/ppermute | solution.py:697
  186.1 32.0 %collective-permute-start.44 = (bf16[3,272,768]{2,1,0:T(8,128)(2,1)S(1)}, bf16[3,272,768]{2,1,0:T(8,128)(2,1)}, u32[]{:S(2)}, u32[]{:S(2)}) collective-permute-start(bf16[3,272,768]{2,1,0:T(8,128)(2,1)S(1)} %add_convert_fusion.zm_ref), channel_id=1, source_target_pairs={{0,1},{1,0},{2,3},{3,2},{4,5},{5,4},{6,7},{7,6},{8,9},{9,8},{10,11... | collective-permute-start | bytes 3760136 | tf_op jit(solution)/shard_map/ppermute | solution.py:725
  187.4 30.6 %collective-permute-start.45 = (bf16[4,3,48,768]{3,2,1,0:T(8,128)(2,1)}, bf16[4,3,48,768]{3,2,1,0:T(8,128)(2,1)}, u32[]{:S(2)}, u32[]{:S(2)}) collective-permute-start(bf16[4,3,48,768]{3,2,1,0:T(8,128)(2,1)} %get-tuple-element.185), channel_id=1, source_target_pairs={{0,4},{2,6},{4,0},{6,2},{8,12},{10,14},{12,8},{14,10},{16,20},{18,... | collective-permute-start | bytes 2654216 | tf_op jit(solution)/shard_map/ppermute | solution.py:697
  188.2 32.0 %collective-permute-start.46 = (bf16[2,3,48,768]{3,2,1,0:T(8,128)(2,1)}, bf16[2,3,48,768]{3,2,1,0:T(8,128)(2,1)}, u32[]{:S(2)}, u32[]{:S(2)}) collective-permute-start(bf16[2,3,48,768]{3,2,1,0:T(8,128)(2,1)} %add_convert_fusion.6), channel_id=1, source_target_pairs={{0,8},{2,10},{4,12},{6,14},{8,0},{10,2},{12,4},{14,6},{16,24},{18,... | collective-permute-start | bytes 1327112 | tf_op jit(solution)/shard_map/ppermute | solution.py:697
  189.9 38.2 %collective-permute-start.48 = (bf16[4,3,48,768]{3,2,1,0:T(8,128)(2,1)}, bf16[4,3,48,768]{3,2,1,0:T(8,128)(2,1)}, u32[]{:S(2)}, u32[]{:S(2)}) collective-permute-start(bf16[4,3,48,768]{3,2,1,0:T(8,128)(2,1)} %get-tuple-element.191), channel_id=1, source_target_pairs={{0,4},{2,6},{4,0},{6,2},{8,12},{10,14},{12,8},{14,10},{16,20},{18,... | collective-permute-start | bytes 2654216 | tf_op jit(solution)/shard_map/ppermute | solution.py:697
  223.7 17.6 %collective-permute-start.54 = (bf16[3,48,768]{2,1,0:T(8,128)(2,1)}, bf16[3,48,768]{2,1,0:T(8,128)(2,1)}, u32[]{:S(2)}, u32[]{:S(2)}) collective-permute-start(bf16[3,48,768]{2,1,0:T(8,128)(2,1)} %fusion.2), channel_id=1, source_target_pairs={{0,16},{2,18},{4,20},{6,22},{8,24},{10,26},{12,28},{14,30},{16,0},... | collective-permute-start | bytes 663560 | tf_op jit(solution)/shard_map/ppermute | solution.py:697
  228.1 18.0 %collective-permute-start.53 = (bf16[2,3,48,768]{3,2,1,0:T(8,128)(2,1)}, bf16[2,3,48,768]{3,2,1,0:T(8,128)(2,1)}, u32[]{:S(2)}, u32[]{:S(2)}) collective-permute-start(bf16[2,3,48,768]{3,2,1,0:T(8,128)(2,1)} %add_convert_fusion.5), channel_id=1, source_target_pairs={{0,8},{2,10},{4,12},{6,14},{8,0},{10,2},{12,4},{14,6},{16,24},{18,... | collective-permute-start | bytes 1327112 | tf_op jit(solution)/shard_map/ppermute | solution.py:697
  229.8 34.6 %collective-permute-start.51 = (bf16[3,272,768]{2,1,0:T(8,128)(2,1)S(1)}, bf16[3,272,768]{2,1,0:T(8,128)(2,1)}, u32[]{:S(2)}, u32[]{:S(2)}) collective-permute-start(bf16[3,272,768]{2,1,0:T(8,128)(2,1)S(1)} %copy-done.19), channel_id=1, source_target_pairs={{0,1},{1,0},{2,3},{3,2},{4,5},{5,4},{6,7},{7,6},{8,9},{9,8},{10,11... | collective-permute-start | bytes 3760136 | tf_op jit(solution)/shard_map/ppermute | solution.py:725
  235.7 17.8 %collective-permute-start.56 = (bf16[2,3,48,768]{3,2,1,0:T(8,128)(2,1)}, bf16[2,3,48,768]{3,2,1,0:T(8,128)(2,1)S(1)}, u32[]{:S(2)}, u32[]{:S(2)}) collective-permute-start(bf16[2,3,48,768]{3,2,1,0:T(8,128)(2,1)} %add_convert_fusion.4), channel_id=1, source_target_pairs={{0,8},{2,10},{4,12},{6,14},{8,0},{10,2},{12,4},{14,6},{16,24},{18,... | collective-permute-start | bytes 1327112 | tf_op jit(solution)/shard_map/ppermute | solution.py:697
  241.3 23.2 %collective-permute-start.57 = (bf16[4,4,48,384]{3,2,1,0:T(8,128)(2,1)S(1)}, bf16[4,4,48,384]{3,2,1,0:T(8,128)(2,1)S(1)}, u32[]{:S(2)}, u32[]{:S(2)}) collective-permute-start(bf16[4,4,48,384]{3,2,1,0:T(8,128)(2,1)S(1)} %copy-done.36), channel_id=1, source_target_pairs={{0,4},{2,6},{4,0},{6,2},{8,12},{10,14},{12,8},{14,10},{16,20},{18,... | collective-permute-start | bytes 1769480 | tf_op jit(solution)/shard_map/ppermute | solution.py:697
  249.5 25.9 %collective-permute-start.59 = (bf16[3,48,768]{2,1,0:T(8,128)(2,1)}, bf16[3,48,768]{2,1,0:T(8,128)(2,1)}, u32[]{:S(2)}, u32[]{:S(2)}) collective-permute-start(bf16[3,48,768]{2,1,0:T(8,128)(2,1)} %fusion.3), channel_id=1, source_target_pairs={{0,16},{2,18},{4,20},{6,22},{8,24},{10,26},{12,28},{14,30},{16,0},... | collective-permute-start | bytes 663560 | tf_op jit(solution)/shard_map/ppermute | solution.py:697
  264.2 18.6 %collective-permute-start.62 = (bf16[3,48,768]{2,1,0:T(8,128)(2,1)}, bf16[3,48,768]{2,1,0:T(8,128)(2,1)}, u32[]{:S(2)}, u32[]{:S(2)}) collective-permute-start(bf16[3,48,768]{2,1,0:T(8,128)(2,1)} %fusion.4), channel_id=1, source_target_pairs={{0,16},{2,18},{4,20},{6,22},{8,24},{10,26},{12,28},{14,30},{16,0},... | collective-permute-start | bytes 663560 | tf_op jit(solution)/shard_map/ppermute | solution.py:697
  (115 other events, 1165.9 us)

commit v3 on v2

--- a/solution.py
+++ b/solution.py
@@ -719,7 +719,7 @@
     me = lax.axis_index("dp")
     core = me % 2
     by_permute = dp == 16 and share % SUB == 0
-    masks = [m for m in (1, 128, 64, 32, 16, 8, 4, 2) if m < dp]
+    masks = [m for m in (1, 4, 128, 64, 32, 16, 8, 2) if m < dp]
 
     def peer(value):
         return lax.ppermute(value, "rep", [(i, i ^ 1) for i in range(rep)])

time: 296 us -> 291 us (0.983)
  waiting for transfers between devices: 65.7 us -> 58.4 us
    ppermute x60, waiting for transfers between devices: 62.7 us -> 55.5 us  [swap(): return lax.ppermute(value, axis, [(i, i ^ mask) for i in range(size)])]
  transfers between devices with their start and end apart: 66 -> 66, of which waited for: 24 -> 25; matrix products, arithmetic and copies ran while one was open for 15% -> 15% of each run, Pallas kernels for 42% -> 43%
where the time goes in v3:
time: 291 us; the launch traced here: 289 us
  Pallas kernels  123 us (42%)
  waiting for transfers between devices  58.4 us (20%)
  starting transfers between devices  52.2 us (18%)
  other arithmetic  34.6 us (12%)
  local copies, waits for them, and re-layouts  19.2 us (7%)
    ppermute x60, waiting for transfers between devices, swap(): return lax.ppermute(value, axis, [(i, i ^ mask) for i in range(size)])  55.5 us
    ppermute x60, starting transfers between devices, swap(): return lax.ppermute(value, axis, [(i, i ^ mask) for i in range(size)])  46.1 us
    pallas_call x1, Pallas kernels, attend_back(): pl.pallas_call(functools.partial(k_attend_back, scale=scale), grid_spec=g...  26.8 us
    pallas_call x2, Pallas kernels, weight_grad(): pl.pallas_call(functools.partial(k_weight_grad, n_left=len(left), n_out=n...  26.4 us
    pallas_call x1, Pallas kernels, experts_back(): pl.pallas_call(functools.partial(k_back, n_left=len(left), n_up=len(ups),...  15.9 us
    pallas_call x1, Pallas kernels, experts_down(): pl.pallas_call(functools.partial(k_down, own=own), grid_spec=grid_spec, o...  10.8 us
    pallas_call x1, Pallas kernels, experts_up(): pl.pallas_call(functools.partial(k_up, n_left=len(b)), grid_spec=grid_spe...  10.2 us
    pallas_call x1, Pallas kernels, project(): pl.pallas_call(k_proj, grid_spec=grid_spec, out_shape=[jax.ShapeDtypeStru...  8.75 us
  transfers between devices with their start and end apart: 66, of which 25 were waited for; matrix products, arithmetic and copies ran while one was open for 15% of the time, Pallas kernels for 43%

profile of v3, /device:TPU:0, one launch (start us, length us, event | category | flops | bytes accessed | tf_op | source)
XLA Modules:
  0.0 289.3 jit_solution(10861389277861140325)
XLA Ops:
  2.2 3.8 %collective-permute-start.2 = (bf16[1,4,48,384]{3,2,1,0:T(8,128)(2,1)S(1)}, bf16[1,4,48,384]{3,2,1,0:T(8,128)(2,1)S(1)}, u32[]{:S(2)}, u32[]{:S(2)}) collective-permute-start(bf16[1,4,48,384]{3,2,1,0:T(8,128)(2,1)S(1)} %maximum_bitcast_fusion.rest_0_), channel_id=1, source_target_pairs={{0,16},{2,18},{4,20},{6,22},{8,24},{10,26},{12,28},{14,30},{16,0},... | collective-permute-start | bytes 442376 | tf_op jit(solution)/shard_map/ppermute | solution.py:697
  10.3 3.4 %collective-permute-done.2.rest_2_ = bf16[1,4,48,384]{3,2,1,0:T(8,128)(2,1)S(1)} collective-permute-done((bf16[1,4,48,384]{3,2,1,0:T(8,128)(2,1)S(1)}, bf16[1,4,48,384]{3,2,1,0:T(8,128)(2,1)S(1)}, u32[]{:S(2)}, u32[]{:S(2)}) %collective-permute-start.2) | collective-permute-done | bytes 147488 | tf_op jit(solution)/shard_map/ppermute | solution.py:697
  36.2 8.8 %project.1 = (bf16[3,272,768]{2,1,0:T(8,128)(2,1)}, bf16[3,3,272,384]{3,2,1,0:T(8,128)(2,1)}, bf16[3,768,384]{2,1,0:T(8,128)(2,1)}, bf16[1,768,384]{2,1,0:T(8,128)(2,1)}) custom-call(s32[16]{0:T(128)} %xor_multiply_fusion.2.off_ref, bf16[3,272,768]{2,1,0:T(8,128)(2,1)} %pad.10.tok_ref, f32[5,768]{1,0:T(8,128)} %stack.48.vec_ref, ...), custom_call_target="tpu_custom_call" | custom-call | flops 1 | bytes 1 | tf_op jit(solution)/shard_map/project/pallas_call | solution.py:138
  44.9 5.7 %collective-permute-done.17.rest_3_ = bf16[2,3,48,768]{3,2,1,0:T(8,128)(2,1)S(1)} collective-permute-done((bf16[2,3,48,768]{3,2,1,0:T(8,128)(2,1)S(1)}, bf16[2,3,48,768]{3,2,1,0:T(8,128)(2,1)S(1)}, u32[]{:S(2)}, u32[]{:S(2)}) %collective-permute-start.17) | collective-permute-done | bytes 442400 | tf_op jit(solution)/shard_map/ppermute | solution.py:697
  59.1 8.3 %attend.1.cm_ref.c_ref = bf16[3,272,384]{2,1,0:T(8,128)(2,1)} custom-call(s32[3]{0:T(128)} %len_ref.1, bf16[3,3,272,384]{3,2,1,0:T(8,128)(2,1)} %get-tuple-element.128.q_ref.k_ref.v_ref, bf16[3,3,272,384]{3,2,1,0:T(8,128)(2,1)} %get-tuple-element.128.q_ref.k_ref.v_ref, bf16[3,3,272,384]{3,2,1,0:T(8,128)(2,1)} %get-tuple-element.128.q_ref.k_ref.v_ref), custom_call_target="tpu_custom_call" | custom-call | flops 1 | bytes 1 | tf_op jit(solution)/shard_map/attend/pallas_call | solution.py:183
  77.8 3.8 %collective-permute-done.28.rest_8_ = bf16[2,3,48,768]{3,2,1,0:T(8,128)(2,1)S(1)} collective-permute-done((bf16[2,3,48,768]{3,2,1,0:T(8,128)(2,1)S(1)}, bf16[2,3,48,768]{3,2,1,0:T(8,128)(2,1)S(1)}, u32[]{:S(2)}, u32[]{:S(2)}) %collective-permute-start.28) | collective-permute-done | bytes 442400 | tf_op jit(solution)/shard_map/ppermute | solution.py:697
  81.6 2.8 collective-permute-done.26.cp_ref
  85.2 5.5 %residual.1 = (f32[3,272,768]{2,1,0:T(8,128)}, bf16[3,272,768]{2,1,0:T(8,128)(2,1)}) custom-call(bf16[3,272,768]{2,1,0:T(8,128)(2,1)} %pad.10.tok_ref, bf16[3,272,384]{2,1,0:T(8,128)(2,1)} %attend.1.cm_ref.c_ref, bf16[3,272,384]{2,1,0:T(8,128)(2,1)} %copy-done.33, bf16[1,768,384]{2,1,0:T(8,128)(2,1)} %get-tuple-element.122.wm_ref.wo_ref, ...), custom_call_target="tpu_custom_call" | custom-call | flops 1 | bytes 1 | tf_op jit(solution)/shard_map/residual/pallas_call | solution.py:204
  98.3 10.2 %experts_up.1 = (bf16[6,288,768]{2,1,0:T(8,128)(2,1)}, bf16[6,288,768]{2,1,0:T(8,128)(2,1)}) custom-call(s32[2,6]{1,0:T(2,128)} %pad_add_fusion.1.e_ref, s32[16]{0:T(128)} %xor_multiply_fusion.1.off_ref, f32[3,768]{1,0:T(4,128)} %constant_dynamic-slice_fusion.bias_ref, bf16[3,272,768]{2,1,0:T(8,128)(2,1)} %get-tuple-element.143.rest_0_, ...), custom_call_target="tpu_custom_call" | custom-call | flops 1 | bytes 1 | tf_op jit(solution)/shard_map/experts_up/pallas_call | solution.py:328
  109.6 13.2 %weight_grad.2 = (bf16[4,3,48,768]{3,2,1,0:T(8,128)(2,1)}, bf16[4,3,48,768]{3,2,1,0:T(8,128)(2,1)}, bf16[4,3,48,768]{3,2,1,0:T(8,128)(2,1)}, bf16[4,3,48,768]{3,2,1,0:T(8,128)(2,1)}, f32[3,768]{1,0:T(4,128)}) custom-call(s32[2,6]{1,0:T(2,128)} %pad_add_fusion.1.e_ref, s32[16]{0:T(128)} %fusion.6.slot_ref, ...), custom_call_target="tpu_custom_call" | custom-call | flops 1 | bytes 1 | tf_op jit(solution)/shard_map/weight_grad/pallas_call | solution.py:387
  125.7 15.9 %experts_back.1 = (bf16[3,272,768]{2,1,0:T(8,128)(2,1)}, bf16[3,272,768]{2,1,0:T(8,128)(2,1)}, bf16[6,288,768]{2,1,0:T(8,128)(2,1)}, f32[3,768]{1,0:T(4,128)}) custom-call(s32[2,6]{1,0:T(2,128)} %pad_add_fusion.1.e_ref, s32[16]{0:T(128)} %xor_multiply_fusion.off_ref, bf16[6,288,768]{2,1,0:T(8,128)(2,1)} %get-tuple-element.156.slope_ref, ...), custom_call_target="tpu_custom_call" | custom-call | flops 1 | bytes 1 | tf_op jit(solution)/shard_map/experts_back/pallas_call | solution.py:474
  141.6 4.5 %collective-permute-done.37 = bf16[4,3,48,768]{3,2,1,0:T(8,128)(2,1)S(1)} collective-permute-done((bf16[4,3,48,768]{3,2,1,0:T(8,128)(2,1)}, bf16[4,3,48,768]{3,2,1,0:T(8,128)(2,1)S(1)}, u32[]{:S(2)}, u32[]{:S(2)}) %collective-permute-start.37) | collective-permute-done | bytes 884768 | tf_op jit(solution)/shard_map/ppermute | solution.py:697
  147.0 3.2 %collective-permute-done.38 = bf16[3,272,768]{2,1,0:T(8,128)(2,1)S(1)} collective-permute-done((bf16[3,272,768]{2,1,0:T(8,128)(2,1)}, bf16[3,272,768]{2,1,0:T(8,128)(2,1)S(1)}, u32[]{:S(2)}, u32[]{:S(2)}) %collective-permute-start.38) | collective-permute-done | bytes 1253408 | tf_op jit(solution)/shard_map/ppermute | solution.py:697
  154.3 13.2 %weight_grad.3 = (bf16[4,3,48,768]{3,2,1,0:T(8,128)(2,1)}, bf16[4,3,48,768]{3,2,1,0:T(8,128)(2,1)}, bf16[4,3,48,768]{3,2,1,0:T(8,128)(2,1)}, bf16[4,3,48,768]{3,2,1,0:T(8,128)(2,1)}, f32[3,768]{1,0:T(4,128)}) custom-call(s32[2,6]{1,0:T(2,128)} %pad_add_fusion.1.e_ref, s32[16]{0:T(128)} %fusion.6.slot_ref, bf16[6,288,768]{2,1,0:T(8,128)(2,1)} %get-tuple-element.157.right_ref, ...), custom_call_target="tpu_custom_call" | custom-call | flops 1 | bytes 1 | tf_op jit(solution)/shard_map/weight_grad/pallas_call | solution.py:387
  169.2 10.8 %experts_down.1 = (bf16[3,272,768]{2,1,0:T(8,128)(2,1)}, bf16[3,272,768]{2,1,0:T(8,128)(2,1)}) custom-call(s32[2,6]{1,0:T(2,128)} %pad_add_fusion.1.e_ref, s32[16]{0:T(128)} %xor_multiply_fusion.off_ref, bf16[6,288,768]{2,1,0:T(8,128)(2,1)} %get-tuple-element.144.right_ref.act_ref, bf16[2,3,48,768]{3,2,1,0:T(8,128)(2,1)} %copy-done.6, ...), custom_call_target="tpu_custom_call" | custom-call | flops 1 | bytes 1 | tf_op jit(solution)/shard_map/experts_down/pallas_call | solution.py:529
  182.6 3.2 %collective-permute-done.43 = bf16[3,272,768]{2,1,0:T(8,128)(2,1)S(1)} collective-permute-done((bf16[3,272,768]{2,1,0:T(8,128)(2,1)}, bf16[3,272,768]{2,1,0:T(8,128)(2,1)S(1)}, u32[]{:S(2)}, u32[]{:S(2)}) %collective-permute-start.43) | collective-permute-done | bytes 1253408 | tf_op jit(solution)/shard_map/ppermute | solution.py:697
  191.2 26.8 %attend_back.1 = (f32[3,272,768]{2,1,0:T(8,128)}, bf16[3,272,768]{2,1,0:T(8,128)(2,1)}, f32[2,768]{1,0:T(2,128)}, f32[3,768]{1,0:T(4,128)}, f32[2,384]{1,0:T(2,1...) custom-call(s32[3]{0:T(128)} %len_ref.1, ...), custom_call_target="tpu_custom_call" | custom-call | flops 1 | bytes 1 | tf_op jit(solution)/shard_map/attend_back/pallas_call | solution.py:657
  224.9 3.2 %collective-permute-done.48 = bf16[4,3,48,768]{3,2,1,0:T(8,128)(2,1)} collective-permute-done((bf16[4,3,48,768]{3,2,1,0:T(8,128)(2,1)}, bf16[4,3,48,768]{3,2,1,0:T(8,128)(2,1)}, u32[]{:S(2)}, u32[]{:S(2)}) %collective-permute-start.48) | collective-permute-done | bytes 884768 | tf_op jit(solution)/shard_map/ppermute | solution.py:697
  236.4 4.9 %finish_output.1 = bf16[3,261,768]{2,1,0:T(8,128)(2,1)} custom-call(s32[2,3]{1,0:T(2,128)} %copy-done.68, f32[3,272,768]{2,1,0:T(8,128)} %get-tuple-element.138.h_ref, bf16[3,272,768]{2,1,0:T(8,128)(2,1)} %copy-done.2, bf16[3,272,768]{2,1,0:T(8,128)(2,1)} %collective-permute-done.44.zp_ref, f32[3,768]{1,0:T(4,128)} %bias_ref.1), custom_call_target="tpu_custom_call" | custom-call | flops 1 | bytes 1 | tf_op jit(solution)/shard_map/finish_output/pallas_call | solution.py:559
  242.5 3.6 %collective-permute-done.53 = bf16[2,3,48,768]{3,2,1,0:T(8,128)(2,1)} collective-permute-done((bf16[2,3,48,768]{3,2,1,0:T(8,128)(2,1)}, bf16[2,3,48,768]{3,2,1,0:T(8,128)(2,1)}, u32[]{:S(2)}, u32[]{:S(2)}) %collective-permute-start.53) | collective-permute-done | bytes 442400 | tf_op jit(solution)/shard_map/ppermute | solution.py:697
  249.6 3.9 %collective-permute-done.56 = bf16[2,3,48,768]{3,2,1,0:T(8,128)(2,1)S(1)} collective-permute-done((bf16[2,3,48,768]{3,2,1,0:T(8,128)(2,1)}, bf16[2,3,48,768]{3,2,1,0:T(8,128)(2,1)S(1)}, u32[]{:S(2)}, u32[]{:S(2)}) %collective-permute-start.56) | collective-permute-done | bytes 442400 | tf_op jit(solution)/shard_map/ppermute | solution.py:697
  255.4 2.7 collective-permute-done.55
  262.2 5.7 %token_grad.1 = f32[3,261,768]{2,1,0:T(8,128)} custom-call(f32[3,272,768]{2,1,0:T(8,128)} %get-tuple-element.205.dh_ref, bf16[3,272,768]{2,1,0:T(8,128)(2,1)} %get-tuple-element.207.dm_ref, bf16[3,272,768]{2,1,0:T(8,128)(2,1)} %collective-permute-done.51.dp_ref, bf16[3,272,768]{2,1,0:T(8,128)(2,1)} %pad.10.tok_ref, f32[5,768]{1,0:T(8,128)} %stack.48.vec_ref), custom_call_target="tpu_custom_call" | custom-call | flops 1 | bytes 1 | tf_op jit(solution)/shard_map/token_grad/pallas_call | solution.py:684
  277.9 2.9 collective-permute-done.65
  (332 shorter events, 117.9 us)
Async XLA Ops:
  0.7 33.4 %collective-permute-start = (bf16[3,261,768]{2,1,0:T(8,128)(2,1)}, bf16[3,261,768]{2,1,0:T(8,128)(2,1)}, u32[]{:S(2)}, u32[]{:S(2)}) collective-permute-start(bf16[3,261,768]{2,1,0:T(8,128)(2,1)} %param.33), channel_id=1, source_target_pairs={{0,2},{2,0},{4,6},{6,4},{8,10},{10,8},{12,14},{14,12},{16,18},{18,... | collective-permute-start | bytes 3608072 | tf_op jit(solution)/shard_map/ppermute | solution.py:697
  28.5 22.1 %collective-permute-start.17 = (bf16[2,3,48,768]{3,2,1,0:T(8,128)(2,1)S(1)}, bf16[2,3,48,768]{3,2,1,0:T(8,128)(2,1)S(1)}, u32[]{:S(2)}, u32[]{:S(2)}) collective-permute-start(bf16[2,3,48,768]{3,2,1,0:T(8,128)(2,1)S(1)} %pad_maximum_fusion.rest_2_), channel_id=1, source_target_pairs={{0,8},{2,10},{4,12},{6,14},{8,0},{10,2},{12,4},{14,6},{16,24},{18,... | collective-permute-start | bytes 1327112 | tf_op jit(solution)/shard_map/ppermute | solution.py:697
  29.4 21.2 %collective-permute-start.18 = (bf16[2,3,48,768]{3,2,1,0:T(8,128)(2,1)S(1)}, bf16[2,3,48,768]{3,2,1,0:T(8,128)(2,1)S(1)}, u32[]{:S(2)}, u32[]{:S(2)}) collective-permute-start(bf16[2,3,48,768]{3,2,1,0:T(8,128)(2,1)S(1)} %pad_maximum_fusion.rest_2_), channel_id=1, source_target_pairs={{0,16},{2,18},{4,20},{6,22},{8,24},{10,26},{12,28},{14,30},{16,0},... | collective-permute-start | bytes 1327112 | tf_op jit(solution)/shard_map/ppermute | solution.py:697
  31.4 19.2 %collective-permute-start.19 = (bf16[2,3,48,768]{3,2,1,0:T(8,128)(2,1)S(1)}, bf16[2,3,48,768]{3,2,1,0:T(8,128)(2,1)S(1)}, u32[]{:S(2)}, u32[]{:S(2)}) collective-permute-start(bf16[2,3,48,768]{3,2,1,0:T(8,128)(2,1)S(1)} %pad_maximum_fusion.rest_2_), channel_id=1, source_target_pairs={{0,4},{2,6},{4,0},{6,2},{8,12},{10,14},{12,8},{14,10},{16,20},{18,... | collective-permute-start | bytes 1327112 | tf_op jit(solution)/shard_map/ppermute | solution.py:697
  32.3 20.8 %collective-permute-start.21 = (bf16[2,3,48,768]{3,2,1,0:T(8,128)(2,1)S(1)}, bf16[2,3,48,768]{3,2,1,0:T(8,128)(2,1)S(1)}, u32[]{:S(2)}, u32[]{:S(2)}) collective-permute-start(bf16[2,3,48,768]{3,2,1,0:T(8,128)(2,1)S(1)} %pad_maximum_fusion.1.rest_10_.rest_0_), channel_id=1, source_target_pairs={{0,4},{2,6},{4,0},{6,2},{8,12},{10,14},{12,8},{14,10},{16,20},{18,... | collective-permute-start | bytes 1327112 | tf_op jit(solution)/shard_map/ppermute | solution.py:697
  70.0 22.1 %collective-permute-start.30 = (bf16[2,3,48,768]{3,2,1,0:T(8,128)(2,1)S(1)}, bf16[2,3,48,768]{3,2,1,0:T(8,128)(2,1)}, u32[]{:S(2)}, u32[]{:S(2)}) collective-permute-start(bf16[2,3,48,768]{3,2,1,0:T(8,128)(2,1)S(1)} %pad_maximum_fusion.1.rest_10_.rest_0_), channel_id=1, source_target_pairs={{0,16},{2,18},{4,20},{6,22},{8,24},{10,26},{12,28},{14,30},{16,0},... | collective-permute-start | bytes 1327112 | tf_op jit(solution)/shard_map/ppermute | solution.py:697
  71.4 20.9 %collective-permute-start.31 = (bf16[2,3,48,768]{3,2,1,0:T(8,128)(2,1)S(1)}, bf16[2,3,48,768]{3,2,1,0:T(8,128)(2,1)}, u32[]{:S(2)}, u32[]{:S(2)}) collective-permute-start(bf16[2,3,48,768]{3,2,1,0:T(8,128)(2,1)S(1)} %pad_maximum_fusion.1.rest_10_.rest_0_), channel_id=1, source_target_pairs={{0,8},{2,10},{4,12},{6,14},{8,0},{10,2},{12,4},{14,6},{16,24},{18,... | collective-permute-start | bytes 1327112 | tf_op jit(solution)/shard_map/ppermute | solution.py:697
  72.5 19.8 %collective-permute-start.29 = (bf16[2,3,48,768]{3,2,1,0:T(8,128)(2,1)S(1)}, bf16[2,3,48,768]{3,2,1,0:T(8,128)(2,1)S(1)}, u32[]{:S(2)}, u32[]{:S(2)}) collective-permute-start(bf16[2,3,48,768]{3,2,1,0:T(8,128)(2,1)S(1)} %collective-permute-done.24.rest_5_), channel_id=1, source_target_pairs={{0,4},{2,6},{4,0},{6,2},{8,12},{10,14},{12,8},{14,10},{16,20},{18,... | collective-permute-start | bytes 1327112 | tf_op jit(solution)/shard_map/ppermute | solution.py:697
  94.5 28.4 %collective-permute-start.36 = (bf16[2,3,48,768]{3,2,1,0:T(8,128)(2,1)}, bf16[2,3,48,768]{3,2,1,0:T(8,128)(2,1)S(1)}, u32[]{:S(2)}, u32[]{:S(2)}) collective-permute-start(bf16[2,3,48,768]{3,2,1,0:T(8,128)(2,1)} %collective-permute-done.30.rest_12_.rest_2_), channel_id=1, source_target_pairs={{0,4},{2,6},{4,0},{6,2},{8,12},{10,14},{12,8},{14,10},{16,20},{18,... | collective-permute-start | bytes 1327112 | tf_op jit(solution)/shard_map/ppermute | solution.py:697
  108.5 16.4 %collective-permute-start.35 = (bf16[2,3,48,768]{3,2,1,0:T(8,128)(2,1)S(1)}, bf16[2,3,48,768]{3,2,1,0:T(8,128)(2,1)S(1)}, u32[]{:S(2)}, u32[]{:S(2)}) collective-permute-start(bf16[2,3,48,768]{3,2,1,0:T(8,128)(2,1)S(1)} %collective-permute-done.34.rest_13_.rest_3_), channel_id=1, source_target_pairs={{0,4},{2,6},{4,0},{6,2},{8,12},{10,14},{12,8},{14,10},{16,20},{18,... | collective-permute-start | bytes 1327112 | tf_op jit(solution)/shard_map/ppermute | solution.py:697
  124.9 21.1 %collective-permute-start.37 = (bf16[4,3,48,768]{3,2,1,0:T(8,128)(2,1)}, bf16[4,3,48,768]{3,2,1,0:T(8,128)(2,1)S(1)}, u32[]{:S(2)}, u32[]{:S(2)}) collective-permute-start(bf16[4,3,48,768]{3,2,1,0:T(8,128)(2,1)} %get-tuple-element.154), channel_id=1, source_target_pairs={{0,4},{2,6},{4,0},{6,2},{8,12},{10,14},{12,8},{14,10},{16,20},{18,... | collective-permute-start | bytes 2654216 | tf_op jit(solution)/shard_map/ppermute | solution.py:697
  150.5 29.7 %collective-permute-start.40 = (bf16[3,272,768]{2,1,0:T(8,128)(2,1)S(1)}, bf16[3,272,768]{2,1,0:T(8,128)(2,1)S(1)}, u32[]{:S(2)}, u32[]{:S(2)}) collective-permute-start(bf16[3,272,768]{2,1,0:T(8,128)(2,1)S(1)} %add_convert_fusion.1.dm_ref), channel_id=1, source_target_pairs={{0,1},{1,0},{2,3},{3,2},{4,5},{5,4},{6,7},{7,6},{8,9},{9,8},{10,11... | collective-permute-start | bytes 3760136 | tf_op jit(solution)/shard_map/ppermute | solution.py:725
  152.1 27.9 %collective-permute-start.41 = (bf16[4,3,48,768]{3,2,1,0:T(8,128)(2,1)}, bf16[4,3,48,768]{3,2,1,0:T(8,128)(2,1)}, u32[]{:S(2)}, u32[]{:S(2)}) collective-permute-start(bf16[4,3,48,768]{3,2,1,0:T(8,128)(2,1)} %get-tuple-element.171), channel_id=1, source_target_pairs={{0,4},{2,6},{4,0},{6,2},{8,12},{10,14},{12,8},{14,10},{16,20},{18,... | collective-permute-start | bytes 2654216 | tf_op jit(solution)/shard_map/ppermute | solution.py:697
  186.1 32.0 %collective-permute-start.44 = (bf16[3,272,768]{2,1,0:T(8,128)(2,1)S(1)}, bf16[3,272,768]{2,1,0:T(8,128)(2,1)}, u32[]{:S(2)}, u32[]{:S(2)}) collective-permute-start(bf16[3,272,768]{2,1,0:T(8,128)(2,1)S(1)} %add_convert_fusion.zm_ref), channel_id=1, source_target_pairs={{0,1},{1,0},{2,3},{3,2},{4,5},{5,4},{6,7},{7,6},{8,9},{9,8},{10,11... | collective-permute-start | bytes 3760136 | tf_op jit(solution)/shard_map/ppermute | solution.py:725
  187.4 30.6 %collective-permute-start.45 = (bf16[4,3,48,768]{3,2,1,0:T(8,128)(2,1)}, bf16[4,3,48,768]{3,2,1,0:T(8,128)(2,1)}, u32[]{:S(2)}, u32[]{:S(2)}) collective-permute-start(bf16[4,3,48,768]{3,2,1,0:T(8,128)(2,1)} %get-tuple-element.185), channel_id=1, source_target_pairs={{0,4},{2,6},{4,0},{6,2},{8,12},{10,14},{12,8},{14,10},{16,20},{18,... | collective-permute-start | bytes 2654216 | tf_op jit(solution)/shard_map/ppermute | solution.py:697
  188.2 32.0 %collective-permute-start.46 = (bf16[2,3,48,768]{3,2,1,0:T(8,128)(2,1)}, bf16[2,3,48,768]{3,2,1,0:T(8,128)(2,1)}, u32[]{:S(2)}, u32[]{:S(2)}) collective-permute-start(bf16[2,3,48,768]{3,2,1,0:T(8,128)(2,1)} %add_convert_fusion.6), channel_id=1, source_target_pairs={{0,8},{2,10},{4,12},{6,14},{8,0},{10,2},{12,4},{14,6},{16,24},{18,... | collective-permute-start | bytes 1327112 | tf_op jit(solution)/shard_map/ppermute | solution.py:697
  189.9 38.2 %collective-permute-start.48 = (bf16[4,3,48,768]{3,2,1,0:T(8,128)(2,1)}, bf16[4,3,48,768]{3,2,1,0:T(8,128)(2,1)}, u32[]{:S(2)}, u32[]{:S(2)}) collective-permute-start(bf16[4,3,48,768]{3,2,1,0:T(8,128)(2,1)} %get-tuple-element.191), channel_id=1, source_target_pairs={{0,4},{2,6},{4,0},{6,2},{8,12},{10,14},{12,8},{14,10},{16,20},{18,... | collective-permute-start | bytes 2654216 | tf_op jit(solution)/shard_map/ppermute | solution.py:697
  223.7 17.6 %collective-permute-start.54 = (bf16[3,48,768]{2,1,0:T(8,128)(2,1)}, bf16[3,48,768]{2,1,0:T(8,128)(2,1)}, u32[]{:S(2)}, u32[]{:S(2)}) collective-permute-start(bf16[3,48,768]{2,1,0:T(8,128)(2,1)} %fusion.2), channel_id=1, source_target_pairs={{0,16},{2,18},{4,20},{6,22},{8,24},{10,26},{12,28},{14,30},{16,0},... | collective-permute-start | bytes 663560 | tf_op jit(solution)/shard_map/ppermute | solution.py:697
  228.1 18.0 %collective-permute-start.53 = (bf16[2,3,48,768]{3,2,1,0:T(8,128)(2,1)}, bf16[2,3,48,768]{3,2,1,0:T(8,128)(2,1)}, u32[]{:S(2)}, u32[]{:S(2)}) collective-permute-start(bf16[2,3,48,768]{3,2,1,0:T(8,128)(2,1)} %add_convert_fusion.5), channel_id=1, source_target_pairs={{0,8},{2,10},{4,12},{6,14},{8,0},{10,2},{12,4},{14,6},{16,24},{18,... | collective-permute-start | bytes 1327112 | tf_op jit(solution)/shard_map/ppermute | solution.py:697
  229.8 29.4 %collective-permute-start.51 = (bf16[3,272,768]{2,1,0:T(8,128)(2,1)S(1)}, bf16[3,272,768]{2,1,0:T(8,128)(2,1)}, u32[]{:S(2)}, u32[]{:S(2)}) collective-permute-start(bf16[3,272,768]{2,1,0:T(8,128)(2,1)S(1)} %copy-done.19), channel_id=1, source_target_pairs={{0,1},{1,0},{2,3},{3,2},{4,5},{5,4},{6,7},{7,6},{8,9},{9,8},{10,11... | collective-permute-start | bytes 3760136 | tf_op jit(solution)/shard_map/ppermute | solution.py:725
  235.7 17.8 %collective-permute-start.56 = (bf16[2,3,48,768]{3,2,1,0:T(8,128)(2,1)}, bf16[2,3,48,768]{3,2,1,0:T(8,128)(2,1)S(1)}, u32[]{:S(2)}, u32[]{:S(2)}) collective-permute-start(bf16[2,3,48,768]{3,2,1,0:T(8,128)(2,1)} %add_convert_fusion.4), channel_id=1, source_target_pairs={{0,8},{2,10},{4,12},{6,14},{8,0},{10,2},{12,4},{14,6},{16,24},{18,... | collective-permute-start | bytes 1327112 | tf_op jit(solution)/shard_map/ppermute | solution.py:697
  241.3 18.0 %collective-permute-start.57 = (bf16[4,4,48,384]{3,2,1,0:T(8,128)(2,1)S(1)}, bf16[4,4,48,384]{3,2,1,0:T(8,128)(2,1)S(1)}, u32[]{:S(2)}, u32[]{:S(2)}) collective-permute-start(bf16[4,4,48,384]{3,2,1,0:T(8,128)(2,1)S(1)} %copy-done.36), channel_id=1, source_target_pairs={{0,4},{2,6},{4,0},{6,2},{8,12},{10,14},{12,8},{14,10},{16,20},{18,... | collective-permute-start | bytes 1769480 | tf_op jit(solution)/shard_map/ppermute | solution.py:697
  249.5 20.6 %collective-permute-start.59 = (bf16[3,48,768]{2,1,0:T(8,128)(2,1)}, bf16[3,48,768]{2,1,0:T(8,128)(2,1)}, u32[]{:S(2)}, u32[]{:S(2)}) collective-permute-start(bf16[3,48,768]{2,1,0:T(8,128)(2,1)} %fusion.3), channel_id=1, source_target_pairs={{0,16},{2,18},{4,20},{6,22},{8,24},{10,26},{12,28},{14,30},{16,0},... | collective-permute-start | bytes 663560 | tf_op jit(solution)/shard_map/ppermute | solution.py:697
  258.1 19.8 %collective-permute-start.62 = (bf16[3,48,768]{2,1,0:T(8,128)(2,1)}, bf16[3,48,768]{2,1,0:T(8,128)(2,1)}, u32[]{:S(2)}, u32[]{:S(2)}) collective-permute-start(bf16[3,48,768]{2,1,0:T(8,128)(2,1)} %fusion.4), channel_id=1, source_target_pairs={{0,16},{2,18},{4,20},{6,22},{8,24},{10,26},{12,28},{14,30},{16,0},... | collective-permute-start | bytes 663560 | tf_op jit(solution)/shard_map/ppermute | solution.py:697
  (115 other events, 1150.1 us)
